TPU v7x, 32 devices: a whole 2x2x4 slice. The times are simulated.
32 devices in a mesh: frames: 4 (over z), states: 8 (over y, x, core).
Axes of the slice: x: 2, y: 2, z: 4, core: 2. Of those that a mesh axis runs over, the one named last changes fastest.
Arguments:
- features: bfloat16 [2048, 1024], P('states', 'frames'), may hold values from -10 to 10
- state_ids: int32 [2048, 32], P('states'), may hold values from 0 to 767, as said below
- weights: float32 [2048, 32], P('states'), may hold values from 0.05 to 1
Outputs:
- means: bfloat16 [768, 1024], P(None, 'frames')
- precisions: bfloat16 [768, 1024], P(None, 'frames')
- frame_score: float32 [2048], P('states')
Inputs may be any that keep to these rules, and one draw needn't show every extreme that they name: `state_ids`: each row names 32 different states; every state is named by some row.
All inputs are finite; a program needn't handle non-finite values.
Results may differ from a plain program's by a relative error of at most 0.0034.
Values may be sent and summed in bfloat16 or wider, within the bound.
No kernel may reach another device: no remote copies, remote signals or barrier semaphores. Data moves between devices by JAX's collectives and lax.ppermute only.
A program may use at most 128 MiB of HBM per device.

v0:
```python
import functools
import jax
import jax.numpy as jnp
from jax import lax
from jax.experimental import pallas as pl
from jax.experimental.pallas import tpu as pltpu
from jax.sharding import PartitionSpec as P


STATE_DEV = 96
GROUP = 128
variance_floor = 0.25
FAR = (4, 2, 7)


def vmem(n):
    return [pl.BlockSpec(memory_space=pltpu.VMEM)] * n


def swap(value, axis, k):
    n = lax.axis_size(axis)
    return lax.ppermute(value, axis, [(i, i ^ k) for i in range(n)])


def core():
    return lax.axis_index("states") % 2


def prep_kernel(feat_ref, ids_ref, wts_ref, msg_ref, ids_buf, wts_buf, sem):
    rows = feat_ref.shape[0]
    topk = ids_ref.shape[0]
    copies = [
        pltpu.make_async_copy(ids_ref, ids_buf, sem.at[0]),
        pltpu.make_async_copy(wts_ref, wts_buf, sem.at[1]),
        pltpu.make_async_copy(feat_ref, msg_ref.at[:rows], sem.at[2]),
    ]
    for copy in copies:
        copy.start()
    copies[0].wait()
    ids = ids_buf[...]
    codes = (GROUP + (ids & (GROUP - 1))) << (ids >> 7)
    msg_ref[rows + topk :] = codes.astype(jnp.float32).astype(jnp.bfloat16)
    copies[1].wait()
    msg_ref[rows : rows + topk] = wts_buf[...].astype(jnp.bfloat16)
    copies[2].wait()


def prep(features, ids, weights):
    rows, width = features.shape
    topk = ids.shape[0]
    return pl.pallas_call(
        prep_kernel,
        out_shape=jax.ShapeDtypeStruct((rows + 2 * topk, width), jnp.bfloat16),
        in_specs=[pl.BlockSpec(memory_space=pltpu.HBM)] * 3,
        out_specs=vmem(1)[0],
        scratch_shapes=[
            pltpu.VMEM(ids.shape, ids.dtype),
            pltpu.VMEM(weights.shape, weights.dtype),
            pltpu.SemaphoreType.DMA((3,)),
        ],
        compiler_params=pltpu.CompilerParams(vmem_limit_bytes=4 << 20),
        name="prep",
    )(*[pltpu.with_memory_space_constraint(v, pltpu.HBM) for v in (features, ids, weights)])


def build(ref, topk, post_ref, at, occ):
    width = ref.shape[1]
    rows = ref.shape[0] - 2 * topk
    states = post_ref.shape[0]
    groups = states // GROUP
    scale = (1 << (core() * groups)).astype(jnp.float32)
    base = (lax.broadcasted_iota(jnp.int32, (GROUP, 128), 0) + GROUP).astype(jnp.float32) * scale
    for tile in range(width // 128):
        lanes = slice(tile * 128, tile * 128 + 128)
        wts = ref[rows : rows + topk, lanes]
        codes = ref[rows + topk :, lanes]
        for group in range(groups):
            names = (base * float(2 ** group)).astype(jnp.bfloat16)
            acc = jnp.zeros((GROUP, 128), jnp.bfloat16)
            for j in range(topk):
                acc = jnp.where(codes[j : j + 1] == names, wts[j : j + 1], acc)
            post_ref[group * GROUP : (group + 1) * GROUP, at + tile * 128 : at + tile * 128 + 128] = acc
            part = acc.astype(jnp.float32)
            occ[group] = part if occ[group] is None else occ[group] + part


def fill(ref, topk, pair_ref, at):
    width = ref.shape[1]
    rows = ref.shape[0] - 2 * topk
    x = ref[:rows]
    xf = x.astype(jnp.float32)
    pair_ref[at : at + rows, :width] = x
    pair_ref[at : at + rows, width:] = (xf * xf).astype(jnp.bfloat16)


def gather_sums(msgs, topk, post_ref, pair_ref, old_sum, old_occ):
    width = msgs[0].shape[1]
    rows = msgs[0].shape[0] - 2 * topk
    groups = post_ref.shape[0] // GROUP
    occ = [None] * groups
    if old_occ is not None:
        occ = [old_occ[g * GROUP : (g + 1) * GROUP] for g in range(groups)]
    for i, ref in enumerate(msgs):
        build(ref, topk, post_ref, i * width, occ)
        fill(ref, topk, pair_ref, i * rows)
    total = jnp.dot(post_ref[...], pair_ref[...], preferred_element_type=jnp.float32)
    if old_sum is not None:
        total = total + old_sum[...]
    return total, occ


def moments_kernel(n, topk, first, *refs):
    msgs, rest = refs[:n], refs[n:]
    if first:
        sum_ref, occ_ref, post_ref, pair_ref = rest
        old_sum = old_occ = None
    else:
        old_sum, old_occ, sum_ref, occ_ref, post_ref, pair_ref = rest
    total, occ = gather_sums(msgs, topk, post_ref, pair_ref, old_sum, old_occ)
    sum_ref[...] = total
    for g, part in enumerate(occ):
        occ_ref[g * GROUP : (g + 1) * GROUP] = part


def moments(msgs, topk, states, old):
    width = msgs[0].shape[1]
    rows = msgs[0].shape[0] - 2 * topk
    n = len(msgs)
    first = not old
    post = jax.ShapeDtypeStruct((states, n * width), jnp.bfloat16)
    outs = [jax.ShapeDtypeStruct((states, 2 * width), jnp.float32), jax.ShapeDtypeStruct((states, 128), jnp.float32)]
    scratch = [pltpu.VMEM((n * rows, 2 * width), jnp.bfloat16)]
    if first:
        outs.append(post)
    else:
        scratch.insert(0, pltpu.VMEM(post.shape, post.dtype))
    return pl.pallas_call(
        functools.partial(moments_kernel, n, topk, first),
        out_shape=tuple(outs),
        in_specs=vmem(n + len(old)),
        out_specs=tuple(vmem(len(outs))),
        scratch_shapes=scratch,
        compiler_params=pltpu.CompilerParams(vmem_limit_bytes=16 << 20),
        cost_estimate=pl.CostEstimate(flops=states * rows * n * 4000, bytes_accessed=1 << 20, transcendentals=0),
    )(*msgs, *old)


def final_kernel(n, topk, full_width, *refs):
    msgs = refs[:n]
    own_ref, near_ref, own_post_ref, old_sum, old_occ = refs[n : n + 5]
    half_ref, score_ref, post_ref, pair_ref, table_ref, both_ref = refs[n + 5 :]
    width = own_ref.shape[1]
    rows = own_ref.shape[0] - 2 * topk
    states = post_ref.shape[0]
    me = core()
    total, occ = gather_sums(msgs, topk, post_ref, pair_ref, old_sum, old_occ)
    occ = jnp.concatenate(occ, axis=0)
    inverse = 1.0 / jnp.sum(occ, axis=1, keepdims=True)
    mean = total[:, :width] * inverse
    variance = jnp.maximum(total[:, width:] * inverse - mean * mean, variance_floor)
    means = mean.astype(jnp.bfloat16)
    precs = (1.0 / variance).astype(jnp.bfloat16)
    half_ref[:states] = means
    half_ref[states:] = precs
    mean_f = means.astype(jnp.float32)
    prec_f = precs.astype(jnp.float32)
    product = (mean_f * prec_f).astype(jnp.bfloat16).astype(jnp.float32)
    constant = jnp.sum(mean_f * product - jnp.log(prec_f), axis=1, keepdims=True)
    table_ref[:, :width] = (-2.0 * product).astype(jnp.bfloat16)
    table_ref[:, width:] = precs
    fill(own_ref, topk, both_ref, 0)
    fill(near_ref, topk, both_ref, rows)
    likely = lax.dot_general(table_ref[...], both_ref[...], (((1,), (1,)), ((), ())), preferred_element_type=jnp.float32)
    quad = jnp.sum((likely + constant) * own_post_ref[...].astype(jnp.float32), axis=0, keepdims=True)
    for ref, row, at in ((own_ref, me, 0), (near_ref, 1 - me, rows)):
        wsum = jnp.sum(ref[rows : rows + topk].astype(jnp.float32), axis=0, keepdims=True)
        score_ref[pl.ds(row, 1)] = -0.5 * quad[:, at : at + rows] / (full_width * wsum)


def final(msgs, topk, own, near, own_post, old, full_width):
    width = own.shape[1]
    rows = own.shape[0] - 2 * topk
    states = own_post.shape[0]
    n = len(msgs)
    out = jax.ShapeDtypeStruct((2 * states, width), jnp.bfloat16)
    return pl.pallas_call(
        functools.partial(final_kernel, n, topk, float(full_width)),
        out_shape=(out, jax.ShapeDtypeStruct((2, rows), jnp.float32)),
        in_specs=vmem(n + 5),
        out_specs=tuple(vmem(2)),
        scratch_shapes=[
            pltpu.VMEM((states, n * width), jnp.bfloat16),
            pltpu.VMEM((n * rows, 2 * width), jnp.bfloat16),
            pltpu.VMEM((states, 2 * width), jnp.bfloat16),
            pltpu.VMEM((2 * rows, 2 * width), jnp.bfloat16),
        ],
        compiler_params=pltpu.CompilerParams(vmem_limit_bytes=16 << 20),
        cost_estimate=pl.CostEstimate(flops=8 * states * rows * 4 * width, bytes_accessed=4 << 20, transcendentals=0),
        name="final",
    )(*msgs, own, near, own_post, *old)


def place_kernel(mine_ref, other_ref, mean_out, prec_out, sem):
    states = mine_ref.shape[0] // 2
    copies = []
    for i, (ref, where) in enumerate(((mine_ref, core()), (other_ref, 1 - core()))):
        rows = pl.ds(pl.multiple_of(where * states, states), states)
        copies.append(pltpu.make_async_copy(ref.at[:states], mean_out.at[rows], sem.at[2 * i]))
        copies.append(pltpu.make_async_copy(ref.at[states:], prec_out.at[rows], sem.at[2 * i + 1]))
    for copy in copies:
        copy.start()
    for copy in copies:
        copy.wait()


def place(mine, other):
    hbm = pl.BlockSpec(memory_space=pltpu.HBM)
    out = jax.ShapeDtypeStruct(mine.shape, mine.dtype)
    return pl.pallas_call(
        place_kernel,
        out_shape=(out, out),
        in_specs=vmem(2),
        out_specs=(hbm, hbm),
        scratch_shapes=[pltpu.SemaphoreType.DMA((4,))],
        compiler_params=pltpu.CompilerParams(vmem_limit_bytes=4 << 20),
        cost_estimate=pl.CostEstimate(flops=1 << 20, bytes_accessed=1 << 20, transcendentals=0),
        name="place",
    )(mine, other)


def hop(value, pairs):
    return lax.ppermute(value, ("frames", "states"), pairs)


def small_group(features, state_ids, weights):
    return update(features, state_ids, weights)


def update(features, state_ids, weights):
    _, width = features.shape
    topk = state_ids.shape[1]
    group = lax.axis_size("states")
    depth = lax.axis_size("frames")
    states = STATE_DEV * group // 2
    own = prep(features, state_ids.T, weights.T)
    far = [swap(own, "states", k) for k in FAR]
    near = swap(own, "states", 1)
    back = [swap(v, "states", 1) for v in far]
    total, occ, post = moments([own, near], topk, states, ())
    old = moments([far[0]], topk, states, (total, occ))
    old = moments([back[0]], topk, states, old)
    old = moments([far[1]], topk, states, old)
    old = moments([back[1], far[2]], topk, states, old)
    half, score = final([back[2]], topk, own, near, post, old, width * depth)
    score = score + swap(score, "states", 1)
    other = swap(half, "states", 1)
    k = 1
    while k < depth:
        pairs = [(z * group + s, (z ^ k) * group + (s ^ 1)) for z in range(depth) for s in range(group)]
        score = score + hop(score, pairs)
        k *= 2
    means, precisions = place(half, other)
    return means, precisions, jnp.where(core() == 1, score[1], score[0])


def refresh(first, second, counts):
    mean_value = first / counts
    variance = jnp.maximum(second / counts - mean_value * mean_value, variance_floor)
    return (mean_value.astype(jnp.bfloat16), (1.0 / variance).astype(jnp.bfloat16))


def large_group(features, state_ids, weights):
    rows_here, local_width = features.shape
    group_size = lax.axis_size("states")
    full_width = local_width * lax.axis_size("frames")
    total_states = STATE_DEV * group_size
    row_index = jnp.arange(rows_here, dtype=jnp.int32)[:, None]
    rounded = weights.astype(jnp.bfloat16)
    posterior = (
        jnp.zeros((rows_here, total_states), jnp.bfloat16).at[row_index, state_ids].add(rounded)
    )
    values = features.astype(jnp.float32)
    squares = (values * values).astype(jnp.bfloat16)
    blocked = posterior.reshape(rows_here, group_size, STATE_DEV)
    routed = lax.all_to_all(blocked, "states", split_axis=1, concat_axis=0, tiled=True)
    routed = routed.reshape(rows_here * group_size, STATE_DEV)
    owned_counts = jnp.sum(routed, axis=0, dtype=jnp.float32)
    piece = lax.all_gather(features, "states", axis=0, tiled=True)
    piece_f = piece.astype(jnp.float32)
    piece_sq = (piece_f * piece_f).astype(jnp.bfloat16)
    joined = jnp.concatenate([piece, piece_sq], axis=1)
    owned_sums = lax.dot_general(
        routed, joined, (((0,), (0,)), ((), ())), preferred_element_type=jnp.float32
    )
    mean_rows, prec_rows = refresh(
        owned_sums[:, :local_width], owned_sums[:, local_width:], owned_counts[:, None]
    )
    packed = lax.all_gather(
        jnp.concatenate([mean_rows, prec_rows], axis=1), "states", axis=0, tiled=True
    )
    means = packed[:, :local_width]
    precisions = packed[:, local_width:]
    mean_f = means.astype(jnp.float32)
    prec_f = precisions.astype(jnp.float32)
    product = (mean_f * prec_f).astype(jnp.bfloat16)
    constant_term = jnp.sum(mean_f * product.astype(jnp.float32) - jnp.log(prec_f), axis=1)
    lookup_table = jnp.concatenate([precisions, product], axis=1)
    weight_f = rounded.astype(jnp.float32)
    blended = jnp.dot(posterior, lookup_table, preferred_element_type=jnp.float32)
    quadratic = jnp.sum(
        squares.astype(jnp.float32) * blended[:, :local_width]
        - 2.0 * values * blended[:, local_width:],
        axis=1,
    )
    quadratic = quadratic + jnp.sum(weight_f * constant_term[state_ids], axis=1)
    summed = lax.psum(quadratic, "frames")
    weight_sum = jnp.sum(weight_f, axis=1)
    frame_score = -0.5 * summed / (full_width * weight_sum)
    return (means, precisions, frame_score)


def fits(mesh):
    return mesh.shape["states"] == 8 and mesh.shape["frames"] in (2, 4)


def solution(mesh):
    small = fits(mesh)
    return jax.shard_map(
        small_group if small else large_group,
        mesh=mesh,
        in_specs=(P("states", "frames"), P("states", None), P("states", None)),
        out_specs=(P(None, "frames"), P(None, "frames"), P("states")),
        check_vma=False,
    )
```

profile of v0, /device:TPU:0, one launch (start us, length us, event | category | flops | bytes accessed | tf_op | source)
XLA Modules:
  0.0 29.8 jit_solution(4700172456052360469)
XLA Ops:
  0.6 1.0 %prep.1.refs_0_.refs_1_ = bf16[320,256]{1,0:T(8,128)(2,1)S(1)} custom-call(bf16[256,256]{1,0:T(8,128)(2,1)} %feat_ref.1, s32[32,256]{1,0:T(8,128)} %bitcast.3, f32[32,256]{1,0:T(8,128)} %bitcast.4), custom_call_target="tpu_custom_call" | custom-call | tf_op jit(solution)/shard_map/prep/pallas_call | solution.py:51
  1.6 3.1 %collective-permute-start.5 = (bf16[320,256]{1,0:T(8,128)(2,1)S(1)}, bf16[320,256]{1,0:T(8,128)(2,1)S(1)}, u32[]{:S(2)}, u32[]{:S(2)}) collective-permute-start(bf16[320,256]{1,0:T(8,128)(2,1)S(1)} %prep.1.refs_0_.refs_1_), channel_id=1, source_target_pairs={{0,4},{1,5},{2,6},{3,7},{4,0},{5,1},{6,2},{7,3},{8,12},{9,13},{10,... | collective-permute-start | bytes 491528 | tf_op jit(solution)/shard_map/ppermute | solution.py:22
  4.7 1.5 %collective-permute-start.3 = (bf16[320,256]{1,0:T(8,128)(2,1)S(1)}, bf16[320,256]{1,0:T(8,128)(2,1)S(1)}, u32[]{:S(2)}, u32[]{:S(2)}) collective-permute-start(bf16[320,256]{1,0:T(8,128)(2,1)S(1)} %prep.1.refs_0_.refs_1_), channel_id=1, source_target_pairs={{0,2},{1,3},{2,0},{3,1},{4,6},{5,7},{6,4},{7,5},{8,10},{9,11},{10,... | collective-permute-start | bytes 491528 | tf_op jit(solution)/shard_map/ppermute | solution.py:22
  6.2 0.0 collective-permute-start
  6.2 0.2 collective-permute-start.2
  6.3 2.5 %collective-permute-done.5.refs_0_ = bf16[320,256]{1,0:T(8,128)(2,1)S(1)} collective-permute-done((bf16[320,256]{1,0:T(8,128)(2,1)S(1)}, bf16[320,256]{1,0:T(8,128)(2,1)S(1)}, u32[]{:S(2)}, u32[]{:S(2)}) %collective-permute-start.5) | collective-permute-done | bytes 163872 | tf_op jit(solution)/shard_map/ppermute | solution.py:22
  8.9 0.0 collective-permute-start.6
  8.9 2.7 %collective-permute-done.3.refs_0_ = bf16[320,256]{1,0:T(8,128)(2,1)S(1)} collective-permute-done((bf16[320,256]{1,0:T(8,128)(2,1)S(1)}, bf16[320,256]{1,0:T(8,128)(2,1)S(1)}, u32[]{:S(2)}, u32[]{:S(2)}) %collective-permute-start.3) | collective-permute-done | bytes 163872 | tf_op jit(solution)/shard_map/ppermute | solution.py:22
  11.6 0.0 collective-permute-start.4
  11.6 2.0 %collective-permute-done.refs_1_ = bf16[320,256]{1,0:T(8,128)(2,1)S(1)} collective-permute-done((bf16[320,256]{1,0:T(8,128)(2,1)S(1)}, bf16[320,256]{1,0:T(8,128)(2,1)S(1)}, u32[]{:S(2)}, u32[]{:S(2)}) %collective-permute-start) | collective-permute-done | bytes 163872 | tf_op jit(solution)/shard_map/ppermute | solution.py:22
  13.6 0.1 collective-permute-start.1
  13.7 0.0 collective-permute-done.2.refs_1_.refs_2_
  13.7 1.3 %shard_map.58 = (f32[384,512]{1,0:T(8,128)S(1)}, f32[384,128]{1,0:T(8,128)S(1)}, bf16[384,512]{1,0:T(8,128)(2,1)S(1)}) custom-call(bf16[320,256]{1,0:T(8,128)(2,1)S(1)} %prep.1.refs_0_.refs_1_, bf16[320,256]{1,0:T(8,128)(2,1)S(1)} %collective-permute-done.2.refs_1_.refs_2_), custom_call_target="tpu_custom_call" | custom-call | flops 786432000 | bytes 1048576 | tf_op jit(solution)/shard_map/pallas_call | solution.py:137
  14.9 0.7 %shard_map.59 = (f32[384,512]{1,0:T(8,128)S(1)}, f32[384,128]{1,0:T(8,128)S(1)}) custom-call(bf16[320,256]{1,0:T(8,128)(2,1)S(1)} %collective-permute-done.5.refs_0_, f32[384,512]{1,0:T(8,128)S(1)} %get-tuple-element.19.refs_1_, f32[384,128]{1,0:T(8,128)S(1)} %get-tuple-element.20.refs_2_), custom_call_target="tpu_custom_call" | custom-call | flops 393216000 | bytes 1048576 | tf_op jit(solution)/shard_map/pallas_call | solution.py:137
  15.7 0.0 collective-permute-done.6.refs_0_
  15.7 0.7 %shard_map.60 = (f32[384,512]{1,0:T(8,128)S(1)}, f32[384,128]{1,0:T(8,128)S(1)}) custom-call(bf16[320,256]{1,0:T(8,128)(2,1)S(1)} %collective-permute-done.6.refs_0_, f32[384,512]{1,0:T(8,128)S(1)} %get-tuple-element.21.refs_1_, f32[384,128]{1,0:T(8,128)S(1)} %get-tuple-element.22.refs_2_), custom_call_target="tpu_custom_call" | custom-call | flops 393216000 | bytes 1048576 | tf_op jit(solution)/shard_map/pallas_call | solution.py:137
  16.4 0.7 %shard_map.61 = (f32[384,512]{1,0:T(8,128)S(1)}, f32[384,128]{1,0:T(8,128)S(1)}) custom-call(bf16[320,256]{1,0:T(8,128)(2,1)S(1)} %collective-permute-done.3.refs_0_, f32[384,512]{1,0:T(8,128)S(1)} %get-tuple-element.23.refs_1_, f32[384,128]{1,0:T(8,128)S(1)} %get-tuple-element.24.refs_2_), custom_call_target="tpu_custom_call" | custom-call | flops 393216000 | bytes 1048576 | tf_op jit(solution)/shard_map/pallas_call | solution.py:137
  17.1 0.0 collective-permute-done.4.refs_0_
  17.1 1.3 %shard_map.62 = (f32[384,512]{1,0:T(8,128)S(1)}, f32[384,128]{1,0:T(8,128)S(1)}) custom-call(bf16[320,256]{1,0:T(8,128)(2,1)S(1)} %collective-permute-done.4.refs_0_, bf16[320,256]{1,0:T(8,128)(2,1)S(1)} %collective-permute-done.refs_1_, f32[384,512]{1,0:T(8,128)S(1)} %get-tuple-element.25.refs_2_, f32[384,128]{1,0:T(8,128)S(1)} %get-tuple-element.26.refs_3_), custom_call_target="tpu_custom_call" | custom-call | flops 786432000 | bytes 1048576 | tf_op jit(solution)/shard_map/pallas_call | solution.py:137
  18.4 0.0 collective-permute-done.1.refs_0_
  18.4 1.2 %final.1 = (bf16[768,256]{1,0:T(8,128)(2,1)S(1)}, f32[2,256]{1,0:T(2,128)S(1)}) custom-call(bf16[320,256]{1,0:T(8,128)(2,1)S(1)} %collective-permute-done.1.refs_0_, bf16[320,256]{1,0:T(8,128)(2,1)S(1)} %prep.1.refs_0_.refs_1_, bf16[320,256]{1,0:T(8,128)(2,1)S(1)} %collective-permute-done.2.refs_1_.refs_2_, bf16[384,512]{1,0:T(8,128)(2,1)S(1)} %get-tuple-element.18.refs_3_, ...), custom_call_target="tpu_custom_call" | custom-call | flops 805306368 | bytes 4194304 | tf_op jit(solution)/shard_map/final/pallas_call | solution.py:186
  19.6 0.5 %collective-permute-start.7 = (bf16[768,256]{1,0:T(8,128)(2,1)S(1)}, bf16[768,256]{1,0:T(8,128)(2,1)S(1)}, u32[]{:S(2)}, u32[]{:S(2)}) collective-permute-start(bf16[768,256]{1,0:T(8,128)(2,1)S(1)} %get-tuple-element.29.mine_ref), channel_id=1, source_target_pairs={{0,1},{1,0},{2,3},{3,2},{4,5},{5,4},{6,7},{7,6},{8,9},{9,8},{10,11... | collective-permute-start | bytes 1179656 | tf_op jit(solution)/shard_map/ppermute | solution.py:22
  20.1 0.1 collective-permute-start.8
  20.2 1.2 %collective-permute-done.8 = f32[2,256]{1,0:T(2,128)S(1)} collective-permute-done((f32[2,256]{1,0:T(2,128)S(1)}, f32[2,256]{1,0:T(2,128)S(1)}, u32[]{:S(2)}, u32[]{:S(2)}) %collective-permute-start.8) | collective-permute-done | bytes 2080 | tf_op jit(solution)/shard_map/ppermute | solution.py:22
  21.4 1.6 %collective-permute-start.9 = (f32[2,256]{1,0:T(2,128)S(1)}, f32[2,256]{1,0:T(2,128)S(1)}, u32[]{:S(2)}, u32[]{:S(2)}) collective-permute-start(f32[2,256]{1,0:T(2,128)S(1)} %add.14), channel_id=1, source_target_pairs={{0,9},{1,8},{2,11},{3,10},{4,13},{5,12},{6,15},{7,14},{8,1},{9,0},... | collective-permute-start | bytes 6152 | tf_op jit(solution)/shard_map/ppermute | solution.py:232
  23.0 1.5 %collective-permute-done.9 = f32[2,256]{1,0:T(2,128)S(1)} collective-permute-done((f32[2,256]{1,0:T(2,128)S(1)}, f32[2,256]{1,0:T(2,128)S(1)}, u32[]{:S(2)}, u32[]{:S(2)}) %collective-permute-start.9) | collective-permute-done | bytes 2080 | tf_op jit(solution)/shard_map/ppermute | solution.py:232
  24.4 2.6 %collective-permute-start.10 = (f32[2,256]{1,0:T(2,128)S(1)}, f32[2,256]{1,0:T(2,128)S(1)}, u32[]{:S(2)}, u32[]{:S(2)}) collective-permute-start(f32[2,256]{1,0:T(2,128)S(1)} %add.15), channel_id=1, source_target_pairs={{0,17},{1,16},{2,19},{3,18},{4,21},{5,20},{6,23},{7,22},{8,25},{9,... | collective-permute-start | bytes 6152 | tf_op jit(solution)/shard_map/ppermute | solution.py:232
  27.0 1.3 %collective-permute-done.10 = f32[2,256]{1,0:T(2,128)S(1)} collective-permute-done((f32[2,256]{1,0:T(2,128)S(1)}, f32[2,256]{1,0:T(2,128)S(1)}, u32[]{:S(2)}, u32[]{:S(2)}) %collective-permute-start.10) | collective-permute-done | bytes 2080 | tf_op jit(solution)/shard_map/ppermute | solution.py:232
  28.4 0.6 %broadcast_select_fusion = f32[1,256]{1,0:T(1,128)} fusion(pred[]{:T(512)S(6)} %eq.5, f32[2,256]{1,0:T(2,128)S(1)} %add.16), kind=kLoop, calls=%fused_computation | loop fusion | flops 256 | bytes 3073 | tf_op jit(solution)/shard_map/jit(_where)/select_n | solution.py:263
  28.9 0.0 collective-permute-done.7.other_ref
  28.9 0.9 %place.1 = (bf16[768,256]{1,0:T(8,128)(2,1)}, bf16[768,256]{1,0:T(8,128)(2,1)}) custom-call(bf16[768,256]{1,0:T(8,128)(2,1)S(1)} %get-tuple-element.29.mine_ref, bf16[768,256]{1,0:T(8,128)(2,1)S(1)} %collective-permute-done.7.other_ref), custom_call_target="tpu_custom_call" | custom-call | flops 1048576 | bytes 1048576 | tf_op jit(solution)/shard_map/place/pallas_call | solution.py:219
  (3 shorter events, 0.0 us)
Async XLA Ops:
  1.6 7.3 %collective-permute-start.5 = (bf16[320,256]{1,0:T(8,128)(2,1)S(1)}, bf16[320,256]{1,0:T(8,128)(2,1)S(1)}, u32[]{:S(2)}, u32[]{:S(2)}) collective-permute-start(bf16[320,256]{1,0:T(8,128)(2,1)S(1)} %prep.1.refs_0_.refs_1_), channel_id=1, source_target_pairs={{0,4},{1,5},{2,6},{3,7},{4,0},{5,1},{6,2},{7,3},{8,12},{9,13},{10,... | collective-permute-start | bytes 491528 | tf_op jit(solution)/shard_map/ppermute | solution.py:22
  4.7 6.9 %collective-permute-start.3 = (bf16[320,256]{1,0:T(8,128)(2,1)S(1)}, bf16[320,256]{1,0:T(8,128)(2,1)S(1)}, u32[]{:S(2)}, u32[]{:S(2)}) collective-permute-start(bf16[320,256]{1,0:T(8,128)(2,1)S(1)} %prep.1.refs_0_.refs_1_), channel_id=1, source_target_pairs={{0,2},{1,3},{2,0},{3,1},{4,6},{5,7},{6,4},{7,5},{8,10},{9,11},{10,... | collective-permute-start | bytes 491528 | tf_op jit(solution)/shard_map/ppermute | solution.py:22
  6.2 7.4 %collective-permute-start = (bf16[320,256]{1,0:T(8,128)(2,1)S(1)}, bf16[320,256]{1,0:T(8,128)(2,1)S(1)}, u32[]{:S(2)}, u32[]{:S(2)}) collective-permute-start(bf16[320,256]{1,0:T(8,128)(2,1)S(1)} %prep.1.refs_0_.refs_1_), channel_id=1, source_target_pairs={{0,7},{1,6},{2,5},{3,4},{4,3},{5,2},{6,1},{7,0},{8,15},{9,14},{10,... | collective-permute-start | bytes 491528 | tf_op jit(solution)/shard_map/ppermute | solution.py:22
  6.2 7.5 %collective-permute-start.2 = (bf16[320,256]{1,0:T(8,128)(2,1)S(1)}, bf16[320,256]{1,0:T(8,128)(2,1)S(1)}, u32[]{:S(2)}, u32[]{:S(2)}) collective-permute-start(bf16[320,256]{1,0:T(8,128)(2,1)S(1)} %prep.1.refs_0_.refs_1_), channel_id=1, source_target_pairs={{0,1},{1,0},{2,3},{3,2},{4,5},{5,4},{6,7},{7,6},{8,9},{9,8},{10,11... | collective-permute-start | bytes 491528 | tf_op jit(solution)/shard_map/ppermute | solution.py:22
  8.9 6.8 %collective-permute-start.6 = (bf16[320,256]{1,0:T(8,128)(2,1)S(1)}, bf16[320,256]{1,0:T(8,128)(2,1)S(1)}, u32[]{:S(2)}, u32[]{:S(2)}) collective-permute-start(bf16[320,256]{1,0:T(8,128)(2,1)S(1)} %collective-permute-done.5.refs_0_), channel_id=1, source_target_pairs={{0,1},{1,0},{2,3},{3,2},{4,5},{5,4},{6,7},{7,6},{8,9},{9,8},{10,11... | collective-permute-start | bytes 491528 | tf_op jit(solution)/shard_map/ppermute | solution.py:22
  11.6 5.6 %collective-permute-start.4 = (bf16[320,256]{1,0:T(8,128)(2,1)S(1)}, bf16[320,256]{1,0:T(8,128)(2,1)S(1)}, u32[]{:S(2)}, u32[]{:S(2)}) collective-permute-start(bf16[320,256]{1,0:T(8,128)(2,1)S(1)} %collective-permute-done.3.refs_0_), channel_id=1, source_target_pairs={{0,1},{1,0},{2,3},{3,2},{4,5},{5,4},{6,7},{7,6},{8,9},{9,8},{10,11... | collective-permute-start | bytes 491528 | tf_op jit(solution)/shard_map/ppermute | solution.py:22
  13.6 4.9 %collective-permute-start.1 = (bf16[320,256]{1,0:T(8,128)(2,1)S(1)}, bf16[320,256]{1,0:T(8,128)(2,1)S(1)}, u32[]{:S(2)}, u32[]{:S(2)}) collective-permute-start(bf16[320,256]{1,0:T(8,128)(2,1)S(1)} %collective-permute-done.refs_1_), channel_id=1, source_target_pairs={{0,1},{1,0},{2,3},{3,2},{4,5},{5,4},{6,7},{7,6},{8,9},{9,8},{10,11... | collective-permute-start | bytes 491528 | tf_op jit(solution)/shard_map/ppermute | solution.py:22
  19.6 9.3 %collective-permute-start.7 = (bf16[768,256]{1,0:T(8,128)(2,1)S(1)}, bf16[768,256]{1,0:T(8,128)(2,1)S(1)}, u32[]{:S(2)}, u32[]{:S(2)}) collective-permute-start(bf16[768,256]{1,0:T(8,128)(2,1)S(1)} %get-tuple-element.29.mine_ref), channel_id=1, source_target_pairs={{0,1},{1,0},{2,3},{3,2},{4,5},{5,4},{6,7},{7,6},{8,9},{9,8},{10,11... | collective-permute-start | bytes 1179656 | tf_op jit(solution)/shard_map/ppermute | solution.py:22
  20.1 1.4 %collective-permute-start.8 = (f32[2,256]{1,0:T(2,128)S(1)}, f32[2,256]{1,0:T(2,128)S(1)}, u32[]{:S(2)}, u32[]{:S(2)}) collective-permute-start(f32[2,256]{1,0:T(2,128)S(1)} %get-tuple-element.32), channel_id=1, source_target_pairs={{0,1},{1,0},{2,3},{3,2},{4,5},{5,4},{6,7},{7,6},{8,9},{9,8},{10,11... | collective-permute-start | bytes 6152 | tf_op jit(solution)/shard_map/ppermute | solution.py:22
  21.4 3.0 %collective-permute-start.9 = (f32[2,256]{1,0:T(2,128)S(1)}, f32[2,256]{1,0:T(2,128)S(1)}, u32[]{:S(2)}, u32[]{:S(2)}) collective-permute-start(f32[2,256]{1,0:T(2,128)S(1)} %add.14), channel_id=1, source_target_pairs={{0,9},{1,8},{2,11},{3,10},{4,13},{5,12},{6,15},{7,14},{8,1},{9,0},... | collective-permute-start | bytes 6152 | tf_op jit(solution)/shard_map/ppermute | solution.py:232
  24.4 3.9 %collective-permute-start.10 = (f32[2,256]{1,0:T(2,128)S(1)}, f32[2,256]{1,0:T(2,128)S(1)}, u32[]{:S(2)}, u32[]{:S(2)}) collective-permute-start(f32[2,256]{1,0:T(2,128)S(1)} %add.15), channel_id=1, source_target_pairs={{0,17},{1,16},{2,19},{3,18},{4,21},{5,20},{6,23},{7,22},{8,25},{9,... | collective-permute-start | bytes 6152 | tf_op jit(solution)/shard_map/ppermute | solution.py:232
where the time goes:
time: 30 us; the launch traced here: 29.8 us
  waiting for transfers between devices  11.3 us (38%)
  starting transfers between devices  9.54 us (32%)
  Pallas kernels  7.79 us (26%)
  between operations  0.66 us (2%)
  other arithmetic  0.58 us (2%)
    ppermute x9, waiting for transfers between devices, swap(): return lax.ppermute(value, axis, [(i, i ^ k) for i in range(n)])  8.47 us
    ppermute x9, starting transfers between devices, swap(): return lax.ppermute(value, axis, [(i, i ^ k) for i in range(n)])  5.41 us
    pallas_call x5, Pallas kernels, moments(): pl.pallas_call(functools.partial(moments_kernel, n, topk, first), out_sha...  4.74 us
    ppermute x2, starting transfers between devices, hop(): return lax.ppermute(value, ('frames', 'states'), pairs)  4.12 us
    ppermute x2, waiting for transfers between devices, hop(): return lax.ppermute(value, ('frames', 'states'), pairs)  2.79 us
    pallas_call x1, Pallas kernels, final(): pl.pallas_call(functools.partial(final_kernel, n, topk, float(full_width)...  1.18 us
    pallas_call x1, Pallas kernels, prep(): pl.pallas_call(prep_kernel, out_shape=jax.ShapeDtypeStruct((rows + 2 * to...  0.97 us
    pallas_call x1, Pallas kernels, place(): pl.pallas_call(place_kernel, out_shape=(out, out), in_specs=vmem(2), out_...  0.9 us
  transfers between devices with their start and end apart: 11, of which 6 were waited for; matrix products, arithmetic and copies ran while one was open for 2% of the time, Pallas kernels for 16%

commit v1 on v0

--- a/solution.py
+++ b/solution.py
@@ -9,6 +9,7 @@
 
 STATE_DEV = 96
 GROUP = 128
+PARTS = 4
 variance_floor = 0.25
 FAR = (4, 2, 7)
 
@@ -32,8 +33,11 @@
     copies = [
         pltpu.make_async_copy(ids_ref, ids_buf, sem.at[0]),
         pltpu.make_async_copy(wts_ref, wts_buf, sem.at[1]),
-        pltpu.make_async_copy(feat_ref, msg_ref.at[:rows], sem.at[2]),
     ]
+    step = rows // PARTS
+    for i in range(PARTS):
+        part = pl.ds(i * step, step)
+        copies.append(pltpu.make_async_copy(feat_ref.at[part], msg_ref.at[part], sem.at[2 + i]))
     for copy in copies:
         copy.start()
     copies[0].wait()
@@ -42,7 +46,8 @@
     msg_ref[rows + topk :] = codes.astype(jnp.float32).astype(jnp.bfloat16)
     copies[1].wait()
     msg_ref[rows : rows + topk] = wts_buf[...].astype(jnp.bfloat16)
-    copies[2].wait()
+    for copy in copies[2:]:
+        copy.wait()
 
 
 def prep(features, ids, weights):
@@ -56,7 +61,7 @@
         scratch_shapes=[
             pltpu.VMEM(ids.shape, ids.dtype),
             pltpu.VMEM(weights.shape, weights.dtype),
-            pltpu.SemaphoreType.DMA((3,)),
+            pltpu.SemaphoreType.DMA((2 + PARTS,)),
         ],
         compiler_params=pltpu.CompilerParams(vmem_limit_bytes=4 << 20),
         name="prep",
@@ -88,9 +93,8 @@
     width = ref.shape[1]
     rows = ref.shape[0] - 2 * topk
     x = ref[:rows]
-    xf = x.astype(jnp.float32)
     pair_ref[at : at + rows, :width] = x
-    pair_ref[at : at + rows, width:] = (xf * xf).astype(jnp.bfloat16)
+    pair_ref[at : at + rows, width:] = x * x
 
 
 def gather_sums(msgs, topk, post_ref, pair_ref, old_sum, old_occ):
@@ -129,11 +133,12 @@
     first = not old
     post = jax.ShapeDtypeStruct((states, n * width), jnp.bfloat16)
     outs = [jax.ShapeDtypeStruct((states, 2 * width), jnp.float32), jax.ShapeDtypeStruct((states, 128), jnp.float32)]
-    scratch = [pltpu.VMEM((n * rows, 2 * width), jnp.bfloat16)]
+    pair = jax.ShapeDtypeStruct((n * rows, 2 * width), jnp.bfloat16)
+    scratch = []
     if first:
-        outs.append(post)
+        outs += [post, pair]
     else:
-        scratch.insert(0, pltpu.VMEM(post.shape, post.dtype))
+        scratch = [pltpu.VMEM(v.shape, v.dtype) for v in (post, pair)]
     return pl.pallas_call(
         functools.partial(moments_kernel, n, topk, first),
         out_shape=tuple(outs),
@@ -147,8 +152,8 @@
 
 def final_kernel(n, topk, full_width, *refs):
     msgs = refs[:n]
-    own_ref, near_ref, own_post_ref, old_sum, old_occ = refs[n : n + 5]
-    half_ref, score_ref, post_ref, pair_ref, table_ref, both_ref = refs[n + 5 :]
+    own_ref, near_ref, own_post_ref, both_ref, old_sum, old_occ = refs[n : n + 6]
+    half_ref, score_ref, post_ref, pair_ref, table_ref = refs[n + 6 :]
     width = own_ref.shape[1]
     rows = own_ref.shape[0] - 2 * topk
     states = post_ref.shape[0]
@@ -164,12 +169,10 @@
     half_ref[states:] = precs
     mean_f = means.astype(jnp.float32)
     prec_f = precs.astype(jnp.float32)
-    product = (mean_f * prec_f).astype(jnp.bfloat16).astype(jnp.float32)
-    constant = jnp.sum(mean_f * product - jnp.log(prec_f), axis=1, keepdims=True)
-    table_ref[:, :width] = (-2.0 * product).astype(jnp.bfloat16)
+    product = (mean_f * prec_f).astype(jnp.bfloat16)
+    constant = jnp.sum(mean_f * product.astype(jnp.float32) - jnp.log(prec_f), axis=1, keepdims=True)
+    table_ref[:, :width] = product * jnp.bfloat16(-2.0)
     table_ref[:, width:] = precs
-    fill(own_ref, topk, both_ref, 0)
-    fill(near_ref, topk, both_ref, rows)
     likely = lax.dot_general(table_ref[...], both_ref[...], (((1,), (1,)), ((), ())), preferred_element_type=jnp.float32)
     quad = jnp.sum((likely + constant) * own_post_ref[...].astype(jnp.float32), axis=0, keepdims=True)
     for ref, row, at in ((own_ref, me, 0), (near_ref, 1 - me, rows)):
@@ -177,7 +180,7 @@
         score_ref[pl.ds(row, 1)] = -0.5 * quad[:, at : at + rows] / (full_width * wsum)
 
 
-def final(msgs, topk, own, near, own_post, old, full_width):
+def final(msgs, topk, own, near, own_post, both, old, full_width):
     width = own.shape[1]
     rows = own.shape[0] - 2 * topk
     states = own_post.shape[0]
@@ -186,18 +189,17 @@
     return pl.pallas_call(
         functools.partial(final_kernel, n, topk, float(full_width)),
         out_shape=(out, jax.ShapeDtypeStruct((2, rows), jnp.float32)),
-        in_specs=vmem(n + 5),
+        in_specs=vmem(n + 6),
         out_specs=tuple(vmem(2)),
         scratch_shapes=[
             pltpu.VMEM((states, n * width), jnp.bfloat16),
             pltpu.VMEM((n * rows, 2 * width), jnp.bfloat16),
             pltpu.VMEM((states, 2 * width), jnp.bfloat16),
-            pltpu.VMEM((2 * rows, 2 * width), jnp.bfloat16),
         ],
         compiler_params=pltpu.CompilerParams(vmem_limit_bytes=16 << 20),
         cost_estimate=pl.CostEstimate(flops=8 * states * rows * 4 * width, bytes_accessed=4 << 20, transcendentals=0),
         name="final",
-    )(*msgs, own, near, own_post, *old)
+    )(*msgs, own, near, own_post, both, *old)
 
 
 def place_kernel(mine_ref, other_ref, mean_out, prec_out, sem):
@@ -246,12 +248,12 @@
     far = [swap(own, "states", k) for k in FAR]
     near = swap(own, "states", 1)
     back = [swap(v, "states", 1) for v in far]
-    total, occ, post = moments([own, near], topk, states, ())
+    total, occ, post, both = moments([own, near], topk, states, ())
     old = moments([far[0]], topk, states, (total, occ))
     old = moments([back[0]], topk, states, old)
     old = moments([far[1]], topk, states, old)
     old = moments([back[1], far[2]], topk, states, old)
-    half, score = final([back[2]], topk, own, near, post, old, width * depth)
+    half, score = final([back[2]], topk, own, near, post, both, old, width * depth)
     score = score + swap(score, "states", 1)
     other = swap(half, "states", 1)
     k = 1

time: 30 us -> 29.8 us (level)
  no operation moved by 1% of the time
where the time goes in v1:
time: 29.8 us; the launch traced here: 29.6 us
  waiting for transfers between devices  11.3 us (38%)
  starting transfers between devices  9.53 us (32%)
  Pallas kernels  7.61 us (26%)
  between operations  0.66 us (2%)
  other arithmetic  0.58 us (2%)
    ppermute x9, waiting for transfers between devices, swap(): return lax.ppermute(value, axis, [(i, i ^ k) for i in range(n)])  8.47 us
    ppermute x9, starting transfers between devices, swap(): return lax.ppermute(value, axis, [(i, i ^ k) for i in range(n)])  5.41 us
    pallas_call x5, Pallas kernels, moments(): pl.pallas_call(functools.partial(moments_kernel, n, topk, first), out_sha...  4.7 us
    ppermute x2, starting transfers between devices, hop(): return lax.ppermute(value, ('frames', 'states'), pairs)  4.12 us
    ppermute x2, waiting for transfers between devices, hop(): return lax.ppermute(value, ('frames', 'states'), pairs)  2.8 us
    pallas_call x1, Pallas kernels, final(): pl.pallas_call(functools.partial(final_kernel, n, topk, float(full_width)...  1.12 us
    pallas_call x1, Pallas kernels, place(): pl.pallas_call(place_kernel, out_shape=(out, out), in_specs=vmem(2), out_...  0.9 us
    pallas_call x1, Pallas kernels, prep(): pl.pallas_call(prep_kernel, out_shape=jax.ShapeDtypeStruct((rows + 2 * to...  0.89 us
  transfers between devices with their start and end apart: 11, of which 6 were waited for; matrix products, arithmetic and copies ran while one was open for 2% of the time, Pallas kernels for 16%

profile of v1, /device:TPU:0, one launch (start us, length us, event | category | flops | bytes accessed | tf_op | source)
XLA Modules:
  0.0 29.6 jit_solution(10821182509279354093)
XLA Ops:
  0.6 0.9 %prep.1.refs_0_.refs_1_ = bf16[320,256]{1,0:T(8,128)(2,1)S(1)} custom-call(bf16[256,256]{1,0:T(8,128)(2,1)} %feat_ref.1, s32[32,256]{1,0:T(8,128)} %bitcast.3, f32[32,256]{1,0:T(8,128)} %bitcast.4), custom_call_target="tpu_custom_call" | custom-call | tf_op jit(solution)/shard_map/prep/pallas_call | solution.py:56
  1.5 3.1 %collective-permute-start.5 = (bf16[320,256]{1,0:T(8,128)(2,1)S(1)}, bf16[320,256]{1,0:T(8,128)(2,1)S(1)}, u32[]{:S(2)}, u32[]{:S(2)}) collective-permute-start(bf16[320,256]{1,0:T(8,128)(2,1)S(1)} %prep.1.refs_0_.refs_1_), channel_id=1, source_target_pairs={{0,4},{1,5},{2,6},{3,7},{4,0},{5,1},{6,2},{7,3},{8,12},{9,13},{10,... | collective-permute-start | bytes 491528 | tf_op jit(solution)/shard_map/ppermute | solution.py:23
  4.6 1.5 %collective-permute-start.3 = (bf16[320,256]{1,0:T(8,128)(2,1)S(1)}, bf16[320,256]{1,0:T(8,128)(2,1)S(1)}, u32[]{:S(2)}, u32[]{:S(2)}) collective-permute-start(bf16[320,256]{1,0:T(8,128)(2,1)S(1)} %prep.1.refs_0_.refs_1_), channel_id=1, source_target_pairs={{0,2},{1,3},{2,0},{3,1},{4,6},{5,7},{6,4},{7,5},{8,10},{9,11},{10,... | collective-permute-start | bytes 491528 | tf_op jit(solution)/shard_map/ppermute | solution.py:23
  6.1 0.0 collective-permute-start
  6.1 0.2 collective-permute-start.2
  6.2 2.5 %collective-permute-done.5.refs_0_ = bf16[320,256]{1,0:T(8,128)(2,1)S(1)} collective-permute-done((bf16[320,256]{1,0:T(8,128)(2,1)S(1)}, bf16[320,256]{1,0:T(8,128)(2,1)S(1)}, u32[]{:S(2)}, u32[]{:S(2)}) %collective-permute-start.5) | collective-permute-done | bytes 163872 | tf_op jit(solution)/shard_map/ppermute | solution.py:23
  8.8 0.0 collective-permute-start.6
  8.8 2.7 %collective-permute-done.3.refs_0_ = bf16[320,256]{1,0:T(8,128)(2,1)S(1)} collective-permute-done((bf16[320,256]{1,0:T(8,128)(2,1)S(1)}, bf16[320,256]{1,0:T(8,128)(2,1)S(1)}, u32[]{:S(2)}, u32[]{:S(2)}) %collective-permute-start.3) | collective-permute-done | bytes 163872 | tf_op jit(solution)/shard_map/ppermute | solution.py:23
  11.5 0.0 collective-permute-start.4
  11.5 2.0 %collective-permute-done.refs_1_ = bf16[320,256]{1,0:T(8,128)(2,1)S(1)} collective-permute-done((bf16[320,256]{1,0:T(8,128)(2,1)S(1)}, bf16[320,256]{1,0:T(8,128)(2,1)S(1)}, u32[]{:S(2)}, u32[]{:S(2)}) %collective-permute-start) | collective-permute-done | bytes 163872 | tf_op jit(solution)/shard_map/ppermute | solution.py:23
  13.5 0.1 collective-permute-start.1
  13.6 0.0 collective-permute-done.2.refs_1_.refs_2_
  13.6 1.2 %shard_map.58 = (f32[384,512]{1,0:T(8,128)S(1)}, f32[384,128]{1,0:T(8,128)S(1)}, bf16[384,512]{1,0:T(8,128)(2,1)S(1)}, bf16[512,512]{1,0:T(8,128)(2,1)S(1)}) custom-call(bf16[320,256]{1,0:T(8,128)(2,1)S(1)} %prep.1.refs_0_.refs_1_, bf16[320,256]{1,0:T(8,128)(2,1)S(1)} %collective-permute-done.2.refs_1_.refs_2_), custom_call_target="tpu_custom_call" | custom-call | flops 786432000 | bytes 1048576 | tf_op jit(solution)/shard_map/pallas_call | solution.py:142
  14.8 0.7 %shard_map.59 = (f32[384,512]{1,0:T(8,128)S(1)}, f32[384,128]{1,0:T(8,128)S(1)}) custom-call(bf16[320,256]{1,0:T(8,128)(2,1)S(1)} %collective-permute-done.5.refs_0_, f32[384,512]{1,0:T(8,128)S(1)} %get-tuple-element.21.refs_1_, f32[384,128]{1,0:T(8,128)S(1)} %get-tuple-element.22.refs_2_), custom_call_target="tpu_custom_call" | custom-call | flops 393216000 | bytes 1048576 | tf_op jit(solution)/shard_map/pallas_call | solution.py:142
  15.6 0.0 collective-permute-done.6.refs_0_
  15.6 0.7 %shard_map.60 = (f32[384,512]{1,0:T(8,128)S(1)}, f32[384,128]{1,0:T(8,128)S(1)}) custom-call(bf16[320,256]{1,0:T(8,128)(2,1)S(1)} %collective-permute-done.6.refs_0_, f32[384,512]{1,0:T(8,128)S(1)} %get-tuple-element.23.refs_1_, f32[384,128]{1,0:T(8,128)S(1)} %get-tuple-element.24.refs_2_), custom_call_target="tpu_custom_call" | custom-call | flops 393216000 | bytes 1048576 | tf_op jit(solution)/shard_map/pallas_call | solution.py:142
  16.3 0.7 %shard_map.61 = (f32[384,512]{1,0:T(8,128)S(1)}, f32[384,128]{1,0:T(8,128)S(1)}) custom-call(bf16[320,256]{1,0:T(8,128)(2,1)S(1)} %collective-permute-done.3.refs_0_, f32[384,512]{1,0:T(8,128)S(1)} %get-tuple-element.25.refs_1_, f32[384,128]{1,0:T(8,128)S(1)} %get-tuple-element.26.refs_2_), custom_call_target="tpu_custom_call" | custom-call | flops 393216000 | bytes 1048576 | tf_op jit(solution)/shard_map/pallas_call | solution.py:142
  17.0 0.0 collective-permute-done.4.refs_0_
  17.0 1.3 %shard_map.62 = (f32[384,512]{1,0:T(8,128)S(1)}, f32[384,128]{1,0:T(8,128)S(1)}) custom-call(bf16[320,256]{1,0:T(8,128)(2,1)S(1)} %collective-permute-done.4.refs_0_, bf16[320,256]{1,0:T(8,128)(2,1)S(1)} %collective-permute-done.refs_1_, f32[384,512]{1,0:T(8,128)S(1)} %get-tuple-element.27.refs_2_, f32[384,128]{1,0:T(8,128)S(1)} %get-tuple-element.28.refs_3_), custom_call_target="tpu_custom_call" | custom-call | flops 786432000 | bytes 1048576 | tf_op jit(solution)/shard_map/pallas_call | solution.py:142
  18.3 0.0 collective-permute-done.1.refs_0_
  18.3 1.1 %final.1 = (bf16[768,256]{1,0:T(8,128)(2,1)S(1)}, f32[2,256]{1,0:T(2,128)S(1)}) custom-call(bf16[320,256]{1,0:T(8,128)(2,1)S(1)} %collective-permute-done.1.refs_0_, bf16[320,256]{1,0:T(8,128)(2,1)S(1)} %prep.1.refs_0_.refs_1_, bf16[320,256]{1,0:T(8,128)(2,1)S(1)} %collective-permute-done.2.refs_1_.refs_2_, bf16[384,512]{1,0:T(8,128)(2,1)S(1)} %get-tuple-element.19.refs_3_, ...), custom_call_target="tpu_custom_call" | custom-call | flops 805306368 | bytes 4194304 | tf_op jit(solution)/shard_map/final/pallas_call | solution.py:189
  19.4 0.5 %collective-permute-start.7 = (bf16[768,256]{1,0:T(8,128)(2,1)S(1)}, bf16[768,256]{1,0:T(8,128)(2,1)S(1)}, u32[]{:S(2)}, u32[]{:S(2)}) collective-permute-start(bf16[768,256]{1,0:T(8,128)(2,1)S(1)} %get-tuple-element.31.mine_ref), channel_id=1, source_target_pairs={{0,1},{1,0},{2,3},{3,2},{4,5},{5,4},{6,7},{7,6},{8,9},{9,8},{10,11... | collective-permute-start | bytes 1179656 | tf_op jit(solution)/shard_map/ppermute | solution.py:23
  19.9 0.1 collective-permute-start.8
  20.0 1.2 %collective-permute-done.8 = f32[2,256]{1,0:T(2,128)S(1)} collective-permute-done((f32[2,256]{1,0:T(2,128)S(1)}, f32[2,256]{1,0:T(2,128)S(1)}, u32[]{:S(2)}, u32[]{:S(2)}) %collective-permute-start.8) | collective-permute-done | bytes 2080 | tf_op jit(solution)/shard_map/ppermute | solution.py:23
  21.2 1.6 %collective-permute-start.9 = (f32[2,256]{1,0:T(2,128)S(1)}, f32[2,256]{1,0:T(2,128)S(1)}, u32[]{:S(2)}, u32[]{:S(2)}) collective-permute-start(f32[2,256]{1,0:T(2,128)S(1)} %add.14), channel_id=1, source_target_pairs={{0,9},{1,8},{2,11},{3,10},{4,13},{5,12},{6,15},{7,14},{8,1},{9,0},... | collective-permute-start | bytes 6152 | tf_op jit(solution)/shard_map/ppermute | solution.py:234
  22.8 1.5 %collective-permute-done.9 = f32[2,256]{1,0:T(2,128)S(1)} collective-permute-done((f32[2,256]{1,0:T(2,128)S(1)}, f32[2,256]{1,0:T(2,128)S(1)}, u32[]{:S(2)}, u32[]{:S(2)}) %collective-permute-start.9) | collective-permute-done | bytes 2080 | tf_op jit(solution)/shard_map/ppermute | solution.py:234
  24.3 2.6 %collective-permute-start.10 = (f32[2,256]{1,0:T(2,128)S(1)}, f32[2,256]{1,0:T(2,128)S(1)}, u32[]{:S(2)}, u32[]{:S(2)}) collective-permute-start(f32[2,256]{1,0:T(2,128)S(1)} %add.15), channel_id=1, source_target_pairs={{0,17},{1,16},{2,19},{3,18},{4,21},{5,20},{6,23},{7,22},{8,25},{9,... | collective-permute-start | bytes 6152 | tf_op jit(solution)/shard_map/ppermute | solution.py:234
  26.8 1.3 %collective-permute-done.10 = f32[2,256]{1,0:T(2,128)S(1)} collective-permute-done((f32[2,256]{1,0:T(2,128)S(1)}, f32[2,256]{1,0:T(2,128)S(1)}, u32[]{:S(2)}, u32[]{:S(2)}) %collective-permute-start.10) | collective-permute-done | bytes 2080 | tf_op jit(solution)/shard_map/ppermute | solution.py:234
  28.2 0.6 %broadcast_select_fusion = f32[1,256]{1,0:T(1,128)} fusion(pred[]{:T(512)S(6)} %eq.5, f32[2,256]{1,0:T(2,128)S(1)} %add.16), kind=kLoop, calls=%fused_computation | loop fusion | flops 256 | bytes 3073 | tf_op jit(solution)/shard_map/jit(_where)/select_n | solution.py:265
  28.7 0.0 collective-permute-done.7.other_ref
  28.7 0.9 %place.1 = (bf16[768,256]{1,0:T(8,128)(2,1)}, bf16[768,256]{1,0:T(8,128)(2,1)}) custom-call(bf16[768,256]{1,0:T(8,128)(2,1)S(1)} %get-tuple-element.31.mine_ref, bf16[768,256]{1,0:T(8,128)(2,1)S(1)} %collective-permute-done.7.other_ref), custom_call_target="tpu_custom_call" | custom-call | flops 1048576 | bytes 1048576 | tf_op jit(solution)/shard_map/place/pallas_call | solution.py:221
  (3 shorter events, 0.0 us)
Async XLA Ops:
  1.5 7.3 %collective-permute-start.5 = (bf16[320,256]{1,0:T(8,128)(2,1)S(1)}, bf16[320,256]{1,0:T(8,128)(2,1)S(1)}, u32[]{:S(2)}, u32[]{:S(2)}) collective-permute-start(bf16[320,256]{1,0:T(8,128)(2,1)S(1)} %prep.1.refs_0_.refs_1_), channel_id=1, source_target_pairs={{0,4},{1,5},{2,6},{3,7},{4,0},{5,1},{6,2},{7,3},{8,12},{9,13},{10,... | collective-permute-start | bytes 491528 | tf_op jit(solution)/shard_map/ppermute | solution.py:23
  4.6 6.9 %collective-permute-start.3 = (bf16[320,256]{1,0:T(8,128)(2,1)S(1)}, bf16[320,256]{1,0:T(8,128)(2,1)S(1)}, u32[]{:S(2)}, u32[]{:S(2)}) collective-permute-start(bf16[320,256]{1,0:T(8,128)(2,1)S(1)} %prep.1.refs_0_.refs_1_), channel_id=1, source_target_pairs={{0,2},{1,3},{2,0},{3,1},{4,6},{5,7},{6,4},{7,5},{8,10},{9,11},{10,... | collective-permute-start | bytes 491528 | tf_op jit(solution)/shard_map/ppermute | solution.py:23
  6.1 7.4 %collective-permute-start = (bf16[320,256]{1,0:T(8,128)(2,1)S(1)}, bf16[320,256]{1,0:T(8,128)(2,1)S(1)}, u32[]{:S(2)}, u32[]{:S(2)}) collective-permute-start(bf16[320,256]{1,0:T(8,128)(2,1)S(1)} %prep.1.refs_0_.refs_1_), channel_id=1, source_target_pairs={{0,7},{1,6},{2,5},{3,4},{4,3},{5,2},{6,1},{7,0},{8,15},{9,14},{10,... | collective-permute-start | bytes 491528 | tf_op jit(solution)/shard_map/ppermute | solution.py:23
  6.1 7.5 %collective-permute-start.2 = (bf16[320,256]{1,0:T(8,128)(2,1)S(1)}, bf16[320,256]{1,0:T(8,128)(2,1)S(1)}, u32[]{:S(2)}, u32[]{:S(2)}) collective-permute-start(bf16[320,256]{1,0:T(8,128)(2,1)S(1)} %prep.1.refs_0_.refs_1_), channel_id=1, source_target_pairs={{0,1},{1,0},{2,3},{3,2},{4,5},{5,4},{6,7},{7,6},{8,9},{9,8},{10,11... | collective-permute-start | bytes 491528 | tf_op jit(solution)/shard_map/ppermute | solution.py:23
  8.8 6.8 %collective-permute-start.6 = (bf16[320,256]{1,0:T(8,128)(2,1)S(1)}, bf16[320,256]{1,0:T(8,128)(2,1)S(1)}, u32[]{:S(2)}, u32[]{:S(2)}) collective-permute-start(bf16[320,256]{1,0:T(8,128)(2,1)S(1)} %collective-permute-done.5.refs_0_), channel_id=1, source_target_pairs={{0,1},{1,0},{2,3},{3,2},{4,5},{5,4},{6,7},{7,6},{8,9},{9,8},{10,11... | collective-permute-start | bytes 491528 | tf_op jit(solution)/shard_map/ppermute | solution.py:23
  11.5 5.5 %collective-permute-start.4 = (bf16[320,256]{1,0:T(8,128)(2,1)S(1)}, bf16[320,256]{1,0:T(8,128)(2,1)S(1)}, u32[]{:S(2)}, u32[]{:S(2)}) collective-permute-start(bf16[320,256]{1,0:T(8,128)(2,1)S(1)} %collective-permute-done.3.refs_0_), channel_id=1, source_target_pairs={{0,1},{1,0},{2,3},{3,2},{4,5},{5,4},{6,7},{7,6},{8,9},{9,8},{10,11... | collective-permute-start | bytes 491528 | tf_op jit(solution)/shard_map/ppermute | solution.py:23
  13.5 4.8 %collective-permute-start.1 = (bf16[320,256]{1,0:T(8,128)(2,1)S(1)}, bf16[320,256]{1,0:T(8,128)(2,1)S(1)}, u32[]{:S(2)}, u32[]{:S(2)}) collective-permute-start(bf16[320,256]{1,0:T(8,128)(2,1)S(1)} %collective-permute-done.refs_1_), channel_id=1, source_target_pairs={{0,1},{1,0},{2,3},{3,2},{4,5},{5,4},{6,7},{7,6},{8,9},{9,8},{10,11... | collective-permute-start | bytes 491528 | tf_op jit(solution)/shard_map/ppermute | solution.py:23
  19.4 9.3 %collective-permute-start.7 = (bf16[768,256]{1,0:T(8,128)(2,1)S(1)}, bf16[768,256]{1,0:T(8,128)(2,1)S(1)}, u32[]{:S(2)}, u32[]{:S(2)}) collective-permute-start(bf16[768,256]{1,0:T(8,128)(2,1)S(1)} %get-tuple-element.31.mine_ref), channel_id=1, source_target_pairs={{0,1},{1,0},{2,3},{3,2},{4,5},{5,4},{6,7},{7,6},{8,9},{9,8},{10,11... | collective-permute-start | bytes 1179656 | tf_op jit(solution)/shard_map/ppermute | solution.py:23
  19.9 1.4 %collective-permute-start.8 = (f32[2,256]{1,0:T(2,128)S(1)}, f32[2,256]{1,0:T(2,128)S(1)}, u32[]{:S(2)}, u32[]{:S(2)}) collective-permute-start(f32[2,256]{1,0:T(2,128)S(1)} %get-tuple-element.34), channel_id=1, source_target_pairs={{0,1},{1,0},{2,3},{3,2},{4,5},{5,4},{6,7},{7,6},{8,9},{9,8},{10,11... | collective-permute-start | bytes 6152 | tf_op jit(solution)/shard_map/ppermute | solution.py:23
  21.2 3.0 %collective-permute-start.9 = (f32[2,256]{1,0:T(2,128)S(1)}, f32[2,256]{1,0:T(2,128)S(1)}, u32[]{:S(2)}, u32[]{:S(2)}) collective-permute-start(f32[2,256]{1,0:T(2,128)S(1)} %add.14), channel_id=1, source_target_pairs={{0,9},{1,8},{2,11},{3,10},{4,13},{5,12},{6,15},{7,14},{8,1},{9,0},... | collective-permute-start | bytes 6152 | tf_op jit(solution)/shard_map/ppermute | solution.py:234
  24.3 3.9 %collective-permute-start.10 = (f32[2,256]{1,0:T(2,128)S(1)}, f32[2,256]{1,0:T(2,128)S(1)}, u32[]{:S(2)}, u32[]{:S(2)}) collective-permute-start(f32[2,256]{1,0:T(2,128)S(1)} %add.15), channel_id=1, source_target_pairs={{0,17},{1,16},{2,19},{3,18},{4,21},{5,20},{6,23},{7,22},{8,25},{9,... | collective-permute-start | bytes 6152 | tf_op jit(solution)/shard_map/ppermute | solution.py:234

commit v2 on v1

--- a/solution.py
+++ b/solution.py
@@ -276,10 +276,16 @@
     group_size = lax.axis_size("states")
     full_width = local_width * lax.axis_size("frames")
     total_states = STATE_DEV * group_size
-    row_index = jnp.arange(rows_here, dtype=jnp.int32)[:, None]
-    rounded = weights.astype(jnp.bfloat16)
-    posterior = (
-        jnp.zeros((rows_here, total_states), jnp.bfloat16).at[row_index, state_ids].add(rounded)
+    rounded = lax.optimization_barrier(weights.astype(jnp.bfloat16))
+    names = jnp.arange(total_states, dtype=jnp.int32)
+
+    def step(j, posterior):
+        chosen = lax.dynamic_slice_in_dim(state_ids, j, 1, axis=1)
+        value = lax.dynamic_slice_in_dim(rounded, j, 1, axis=1)
+        return jnp.where(chosen == names[None, :], value, posterior)
+
+    posterior = lax.fori_loop(
+        0, state_ids.shape[1], step, jnp.zeros((rows_here, total_states), jnp.bfloat16), unroll=8
     )
     values = features.astype(jnp.float32)
     squares = (values * values).astype(jnp.bfloat16)
@@ -306,15 +312,11 @@
     prec_f = precisions.astype(jnp.float32)
     product = (mean_f * prec_f).astype(jnp.bfloat16)
     constant_term = jnp.sum(mean_f * product.astype(jnp.float32) - jnp.log(prec_f), axis=1)
-    lookup_table = jnp.concatenate([precisions, product], axis=1)
+    lookup_table = jnp.concatenate([precisions, product * jnp.bfloat16(-2.0)], axis=1)
+    both = jnp.concatenate([squares, features], axis=1)
+    likely = lax.dot_general(both, lookup_table, (((1,), (1,)), ((), ())), preferred_element_type=jnp.float32)
+    quadratic = jnp.sum((likely + constant_term[None, :]) * posterior.astype(jnp.float32), axis=1)
     weight_f = rounded.astype(jnp.float32)
-    blended = jnp.dot(posterior, lookup_table, preferred_element_type=jnp.float32)
-    quadratic = jnp.sum(
-        squares.astype(jnp.float32) * blended[:, :local_width]
-        - 2.0 * values * blended[:, local_width:],
-        axis=1,
-    )
-    quadratic = quadratic + jnp.sum(weight_f * constant_term[state_ids], axis=1)
     summed = lax.psum(quadratic, "frames")
     weight_sum = jnp.sum(weight_f, axis=1)
     frame_score = -0.5 * summed / (full_width * weight_sum)

time: 29.8 us -> 29.8 us (level)
  no operation moved by 1% of the time
where the time goes in v2:
time: 29.8 us; the launch traced here: 29.6 us
  waiting for transfers between devices  11.3 us (38%)
  starting transfers between devices  9.53 us (32%)
  Pallas kernels  7.61 us (26%)
  between operations  0.66 us (2%)
  other arithmetic  0.58 us (2%)
    ppermute x9, waiting for transfers between devices, swap(): return lax.ppermute(value, axis, [(i, i ^ k) for i in range(n)])  8.47 us
    ppermute x9, starting transfers between devices, swap(): return lax.ppermute(value, axis, [(i, i ^ k) for i in range(n)])  5.41 us
    pallas_call x5, Pallas kernels, moments(): pl.pallas_call(functools.partial(moments_kernel, n, topk, first), out_sha...  4.7 us
    ppermute x2, starting transfers between devices, hop(): return lax.ppermute(value, ('frames', 'states'), pairs)  4.12 us
    ppermute x2, waiting for transfers between devices, hop(): return lax.ppermute(value, ('frames', 'states'), pairs)  2.8 us
    pallas_call x1, Pallas kernels, final(): pl.pallas_call(functools.partial(final_kernel, n, topk, float(full_width)...  1.12 us
    pallas_call x1, Pallas kernels, place(): pl.pallas_call(place_kernel, out_shape=(out, out), in_specs=vmem(2), out_...  0.9 us
    pallas_call x1, Pallas kernels, prep(): pl.pallas_call(prep_kernel, out_shape=jax.ShapeDtypeStruct((rows + 2 * to...  0.89 us
  transfers between devices with their start and end apart: 11, of which 6 were waited for; matrix products, arithmetic and copies ran while one was open for 2% of the time, Pallas kernels for 16%

profile of v2, /device:TPU:0, one launch (start us, length us, event | category | flops | bytes accessed | tf_op | source)
XLA Modules:
  0.0 29.6 jit_solution(10821182509279354093)
XLA Ops:
  0.6 0.9 %prep.1.refs_0_.refs_1_ = bf16[320,256]{1,0:T(8,128)(2,1)S(1)} custom-call(bf16[256,256]{1,0:T(8,128)(2,1)} %feat_ref.1, s32[32,256]{1,0:T(8,128)} %bitcast.3, f32[32,256]{1,0:T(8,128)} %bitcast.4), custom_call_target="tpu_custom_call" | custom-call | tf_op jit(solution)/shard_map/prep/pallas_call | solution.py:56
  1.5 3.1 %collective-permute-start.5 = (bf16[320,256]{1,0:T(8,128)(2,1)S(1)}, bf16[320,256]{1,0:T(8,128)(2,1)S(1)}, u32[]{:S(2)}, u32[]{:S(2)}) collective-permute-start(bf16[320,256]{1,0:T(8,128)(2,1)S(1)} %prep.1.refs_0_.refs_1_), channel_id=1, source_target_pairs={{0,4},{1,5},{2,6},{3,7},{4,0},{5,1},{6,2},{7,3},{8,12},{9,13},{10,... | collective-permute-start | bytes 491528 | tf_op jit(solution)/shard_map/ppermute | solution.py:23
  4.6 1.5 %collective-permute-start.3 = (bf16[320,256]{1,0:T(8,128)(2,1)S(1)}, bf16[320,256]{1,0:T(8,128)(2,1)S(1)}, u32[]{:S(2)}, u32[]{:S(2)}) collective-permute-start(bf16[320,256]{1,0:T(8,128)(2,1)S(1)} %prep.1.refs_0_.refs_1_), channel_id=1, source_target_pairs={{0,2},{1,3},{2,0},{3,1},{4,6},{5,7},{6,4},{7,5},{8,10},{9,11},{10,... | collective-permute-start | bytes 491528 | tf_op jit(solution)/shard_map/ppermute | solution.py:23
  6.1 0.0 collective-permute-start
  6.1 0.2 collective-permute-start.2
  6.2 2.5 %collective-permute-done.5.refs_0_ = bf16[320,256]{1,0:T(8,128)(2,1)S(1)} collective-permute-done((bf16[320,256]{1,0:T(8,128)(2,1)S(1)}, bf16[320,256]{1,0:T(8,128)(2,1)S(1)}, u32[]{:S(2)}, u32[]{:S(2)}) %collective-permute-start.5) | collective-permute-done | bytes 163872 | tf_op jit(solution)/shard_map/ppermute | solution.py:23
  8.8 0.0 collective-permute-start.6
  8.8 2.7 %collective-permute-done.3.refs_0_ = bf16[320,256]{1,0:T(8,128)(2,1)S(1)} collective-permute-done((bf16[320,256]{1,0:T(8,128)(2,1)S(1)}, bf16[320,256]{1,0:T(8,128)(2,1)S(1)}, u32[]{:S(2)}, u32[]{:S(2)}) %collective-permute-start.3) | collective-permute-done | bytes 163872 | tf_op jit(solution)/shard_map/ppermute | solution.py:23
  11.5 0.0 collective-permute-start.4
  11.5 2.0 %collective-permute-done.refs_1_ = bf16[320,256]{1,0:T(8,128)(2,1)S(1)} collective-permute-done((bf16[320,256]{1,0:T(8,128)(2,1)S(1)}, bf16[320,256]{1,0:T(8,128)(2,1)S(1)}, u32[]{:S(2)}, u32[]{:S(2)}) %collective-permute-start) | collective-permute-done | bytes 163872 | tf_op jit(solution)/shard_map/ppermute | solution.py:23
  13.5 0.1 collective-permute-start.1
  13.6 0.0 collective-permute-done.2.refs_1_.refs_2_
  13.6 1.2 %shard_map.58 = (f32[384,512]{1,0:T(8,128)S(1)}, f32[384,128]{1,0:T(8,128)S(1)}, bf16[384,512]{1,0:T(8,128)(2,1)S(1)}, bf16[512,512]{1,0:T(8,128)(2,1)S(1)}) custom-call(bf16[320,256]{1,0:T(8,128)(2,1)S(1)} %prep.1.refs_0_.refs_1_, bf16[320,256]{1,0:T(8,128)(2,1)S(1)} %collective-permute-done.2.refs_1_.refs_2_), custom_call_target="tpu_custom_call" | custom-call | flops 786432000 | bytes 1048576 | tf_op jit(solution)/shard_map/pallas_call | solution.py:142
  14.8 0.7 %shard_map.59 = (f32[384,512]{1,0:T(8,128)S(1)}, f32[384,128]{1,0:T(8,128)S(1)}) custom-call(bf16[320,256]{1,0:T(8,128)(2,1)S(1)} %collective-permute-done.5.refs_0_, f32[384,512]{1,0:T(8,128)S(1)} %get-tuple-element.21.refs_1_, f32[384,128]{1,0:T(8,128)S(1)} %get-tuple-element.22.refs_2_), custom_call_target="tpu_custom_call" | custom-call | flops 393216000 | bytes 1048576 | tf_op jit(solution)/shard_map/pallas_call | solution.py:142
  15.6 0.0 collective-permute-done.6.refs_0_
  15.6 0.7 %shard_map.60 = (f32[384,512]{1,0:T(8,128)S(1)}, f32[384,128]{1,0:T(8,128)S(1)}) custom-call(bf16[320,256]{1,0:T(8,128)(2,1)S(1)} %collective-permute-done.6.refs_0_, f32[384,512]{1,0:T(8,128)S(1)} %get-tuple-element.23.refs_1_, f32[384,128]{1,0:T(8,128)S(1)} %get-tuple-element.24.refs_2_), custom_call_target="tpu_custom_call" | custom-call | flops 393216000 | bytes 1048576 | tf_op jit(solution)/shard_map/pallas_call | solution.py:142
  16.3 0.7 %shard_map.61 = (f32[384,512]{1,0:T(8,128)S(1)}, f32[384,128]{1,0:T(8,128)S(1)}) custom-call(bf16[320,256]{1,0:T(8,128)(2,1)S(1)} %collective-permute-done.3.refs_0_, f32[384,512]{1,0:T(8,128)S(1)} %get-tuple-element.25.refs_1_, f32[384,128]{1,0:T(8,128)S(1)} %get-tuple-element.26.refs_2_), custom_call_target="tpu_custom_call" | custom-call | flops 393216000 | bytes 1048576 | tf_op jit(solution)/shard_map/pallas_call | solution.py:142
  17.0 0.0 collective-permute-done.4.refs_0_
  17.0 1.3 %shard_map.62 = (f32[384,512]{1,0:T(8,128)S(1)}, f32[384,128]{1,0:T(8,128)S(1)}) custom-call(bf16[320,256]{1,0:T(8,128)(2,1)S(1)} %collective-permute-done.4.refs_0_, bf16[320,256]{1,0:T(8,128)(2,1)S(1)} %collective-permute-done.refs_1_, f32[384,512]{1,0:T(8,128)S(1)} %get-tuple-element.27.refs_2_, f32[384,128]{1,0:T(8,128)S(1)} %get-tuple-element.28.refs_3_), custom_call_target="tpu_custom_call" | custom-call | flops 786432000 | bytes 1048576 | tf_op jit(solution)/shard_map/pallas_call | solution.py:142
  18.3 0.0 collective-permute-done.1.refs_0_
  18.3 1.1 %final.1 = (bf16[768,256]{1,0:T(8,128)(2,1)S(1)}, f32[2,256]{1,0:T(2,128)S(1)}) custom-call(bf16[320,256]{1,0:T(8,128)(2,1)S(1)} %collective-permute-done.1.refs_0_, bf16[320,256]{1,0:T(8,128)(2,1)S(1)} %prep.1.refs_0_.refs_1_, bf16[320,256]{1,0:T(8,128)(2,1)S(1)} %collective-permute-done.2.refs_1_.refs_2_, bf16[384,512]{1,0:T(8,128)(2,1)S(1)} %get-tuple-element.19.refs_3_, ...), custom_call_target="tpu_custom_call" | custom-call | flops 805306368 | bytes 4194304 | tf_op jit(solution)/shard_map/final/pallas_call | solution.py:189
  19.4 0.5 %collective-permute-start.7 = (bf16[768,256]{1,0:T(8,128)(2,1)S(1)}, bf16[768,256]{1,0:T(8,128)(2,1)S(1)}, u32[]{:S(2)}, u32[]{:S(2)}) collective-permute-start(bf16[768,256]{1,0:T(8,128)(2,1)S(1)} %get-tuple-element.31.mine_ref), channel_id=1, source_target_pairs={{0,1},{1,0},{2,3},{3,2},{4,5},{5,4},{6,7},{7,6},{8,9},{9,8},{10,11... | collective-permute-start | bytes 1179656 | tf_op jit(solution)/shard_map/ppermute | solution.py:23
  19.9 0.1 collective-permute-start.8
  20.0 1.2 %collective-permute-done.8 = f32[2,256]{1,0:T(2,128)S(1)} collective-permute-done((f32[2,256]{1,0:T(2,128)S(1)}, f32[2,256]{1,0:T(2,128)S(1)}, u32[]{:S(2)}, u32[]{:S(2)}) %collective-permute-start.8) | collective-permute-done | bytes 2080 | tf_op jit(solution)/shard_map/ppermute | solution.py:23
  21.2 1.6 %collective-permute-start.9 = (f32[2,256]{1,0:T(2,128)S(1)}, f32[2,256]{1,0:T(2,128)S(1)}, u32[]{:S(2)}, u32[]{:S(2)}) collective-permute-start(f32[2,256]{1,0:T(2,128)S(1)} %add.14), channel_id=1, source_target_pairs={{0,9},{1,8},{2,11},{3,10},{4,13},{5,12},{6,15},{7,14},{8,1},{9,0},... | collective-permute-start | bytes 6152 | tf_op jit(solution)/shard_map/ppermute | solution.py:234
  22.8 1.5 %collective-permute-done.9 = f32[2,256]{1,0:T(2,128)S(1)} collective-permute-done((f32[2,256]{1,0:T(2,128)S(1)}, f32[2,256]{1,0:T(2,128)S(1)}, u32[]{:S(2)}, u32[]{:S(2)}) %collective-permute-start.9) | collective-permute-done | bytes 2080 | tf_op jit(solution)/shard_map/ppermute | solution.py:234
  24.3 2.6 %collective-permute-start.10 = (f32[2,256]{1,0:T(2,128)S(1)}, f32[2,256]{1,0:T(2,128)S(1)}, u32[]{:S(2)}, u32[]{:S(2)}) collective-permute-start(f32[2,256]{1,0:T(2,128)S(1)} %add.15), channel_id=1, source_target_pairs={{0,17},{1,16},{2,19},{3,18},{4,21},{5,20},{6,23},{7,22},{8,25},{9,... | collective-permute-start | bytes 6152 | tf_op jit(solution)/shard_map/ppermute | solution.py:234
  26.8 1.3 %collective-permute-done.10 = f32[2,256]{1,0:T(2,128)S(1)} collective-permute-done((f32[2,256]{1,0:T(2,128)S(1)}, f32[2,256]{1,0:T(2,128)S(1)}, u32[]{:S(2)}, u32[]{:S(2)}) %collective-permute-start.10) | collective-permute-done | bytes 2080 | tf_op jit(solution)/shard_map/ppermute | solution.py:234
  28.2 0.6 %broadcast_select_fusion = f32[1,256]{1,0:T(1,128)} fusion(pred[]{:T(512)S(6)} %eq.5, f32[2,256]{1,0:T(2,128)S(1)} %add.16), kind=kLoop, calls=%fused_computation | loop fusion | flops 256 | bytes 3073 | tf_op jit(solution)/shard_map/jit(_where)/select_n | solution.py:265
  28.7 0.0 collective-permute-done.7.other_ref
  28.7 0.9 %place.1 = (bf16[768,256]{1,0:T(8,128)(2,1)}, bf16[768,256]{1,0:T(8,128)(2,1)}) custom-call(bf16[768,256]{1,0:T(8,128)(2,1)S(1)} %get-tuple-element.31.mine_ref, bf16[768,256]{1,0:T(8,128)(2,1)S(1)} %collective-permute-done.7.other_ref), custom_call_target="tpu_custom_call" | custom-call | flops 1048576 | bytes 1048576 | tf_op jit(solution)/shard_map/place/pallas_call | solution.py:221
  (3 shorter events, 0.0 us)
Async XLA Ops:
  1.5 7.3 %collective-permute-start.5 = (bf16[320,256]{1,0:T(8,128)(2,1)S(1)}, bf16[320,256]{1,0:T(8,128)(2,1)S(1)}, u32[]{:S(2)}, u32[]{:S(2)}) collective-permute-start(bf16[320,256]{1,0:T(8,128)(2,1)S(1)} %prep.1.refs_0_.refs_1_), channel_id=1, source_target_pairs={{0,4},{1,5},{2,6},{3,7},{4,0},{5,1},{6,2},{7,3},{8,12},{9,13},{10,... | collective-permute-start | bytes 491528 | tf_op jit(solution)/shard_map/ppermute | solution.py:23
  4.6 6.9 %collective-permute-start.3 = (bf16[320,256]{1,0:T(8,128)(2,1)S(1)}, bf16[320,256]{1,0:T(8,128)(2,1)S(1)}, u32[]{:S(2)}, u32[]{:S(2)}) collective-permute-start(bf16[320,256]{1,0:T(8,128)(2,1)S(1)} %prep.1.refs_0_.refs_1_), channel_id=1, source_target_pairs={{0,2},{1,3},{2,0},{3,1},{4,6},{5,7},{6,4},{7,5},{8,10},{9,11},{10,... | collective-permute-start | bytes 491528 | tf_op jit(solution)/shard_map/ppermute | solution.py:23
  6.1 7.4 %collective-permute-start = (bf16[320,256]{1,0:T(8,128)(2,1)S(1)}, bf16[320,256]{1,0:T(8,128)(2,1)S(1)}, u32[]{:S(2)}, u32[]{:S(2)}) collective-permute-start(bf16[320,256]{1,0:T(8,128)(2,1)S(1)} %prep.1.refs_0_.refs_1_), channel_id=1, source_target_pairs={{0,7},{1,6},{2,5},{3,4},{4,3},{5,2},{6,1},{7,0},{8,15},{9,14},{10,... | collective-permute-start | bytes 491528 | tf_op jit(solution)/shard_map/ppermute | solution.py:23
  6.1 7.5 %collective-permute-start.2 = (bf16[320,256]{1,0:T(8,128)(2,1)S(1)}, bf16[320,256]{1,0:T(8,128)(2,1)S(1)}, u32[]{:S(2)}, u32[]{:S(2)}) collective-permute-start(bf16[320,256]{1,0:T(8,128)(2,1)S(1)} %prep.1.refs_0_.refs_1_), channel_id=1, source_target_pairs={{0,1},{1,0},{2,3},{3,2},{4,5},{5,4},{6,7},{7,6},{8,9},{9,8},{10,11... | collective-permute-start | bytes 491528 | tf_op jit(solution)/shard_map/ppermute | solution.py:23
  8.8 6.8 %collective-permute-start.6 = (bf16[320,256]{1,0:T(8,128)(2,1)S(1)}, bf16[320,256]{1,0:T(8,128)(2,1)S(1)}, u32[]{:S(2)}, u32[]{:S(2)}) collective-permute-start(bf16[320,256]{1,0:T(8,128)(2,1)S(1)} %collective-permute-done.5.refs_0_), channel_id=1, source_target_pairs={{0,1},{1,0},{2,3},{3,2},{4,5},{5,4},{6,7},{7,6},{8,9},{9,8},{10,11... | collective-permute-start | bytes 491528 | tf_op jit(solution)/shard_map/ppermute | solution.py:23
  11.5 5.5 %collective-permute-start.4 = (bf16[320,256]{1,0:T(8,128)(2,1)S(1)}, bf16[320,256]{1,0:T(8,128)(2,1)S(1)}, u32[]{:S(2)}, u32[]{:S(2)}) collective-permute-start(bf16[320,256]{1,0:T(8,128)(2,1)S(1)} %collective-permute-done.3.refs_0_), channel_id=1, source_target_pairs={{0,1},{1,0},{2,3},{3,2},{4,5},{5,4},{6,7},{7,6},{8,9},{9,8},{10,11... | collective-permute-start | bytes 491528 | tf_op jit(solution)/shard_map/ppermute | solution.py:23
  13.5 4.8 %collective-permute-start.1 = (bf16[320,256]{1,0:T(8,128)(2,1)S(1)}, bf16[320,256]{1,0:T(8,128)(2,1)S(1)}, u32[]{:S(2)}, u32[]{:S(2)}) collective-permute-start(bf16[320,256]{1,0:T(8,128)(2,1)S(1)} %collective-permute-done.refs_1_), channel_id=1, source_target_pairs={{0,1},{1,0},{2,3},{3,2},{4,5},{5,4},{6,7},{7,6},{8,9},{9,8},{10,11... | collective-permute-start | bytes 491528 | tf_op jit(solution)/shard_map/ppermute | solution.py:23
  19.4 9.3 %collective-permute-start.7 = (bf16[768,256]{1,0:T(8,128)(2,1)S(1)}, bf16[768,256]{1,0:T(8,128)(2,1)S(1)}, u32[]{:S(2)}, u32[]{:S(2)}) collective-permute-start(bf16[768,256]{1,0:T(8,128)(2,1)S(1)} %get-tuple-element.31.mine_ref), channel_id=1, source_target_pairs={{0,1},{1,0},{2,3},{3,2},{4,5},{5,4},{6,7},{7,6},{8,9},{9,8},{10,11... | collective-permute-start | bytes 1179656 | tf_op jit(solution)/shard_map/ppermute | solution.py:23
  19.9 1.4 %collective-permute-start.8 = (f32[2,256]{1,0:T(2,128)S(1)}, f32[2,256]{1,0:T(2,128)S(1)}, u32[]{:S(2)}, u32[]{:S(2)}) collective-permute-start(f32[2,256]{1,0:T(2,128)S(1)} %get-tuple-element.34), channel_id=1, source_target_pairs={{0,1},{1,0},{2,3},{3,2},{4,5},{5,4},{6,7},{7,6},{8,9},{9,8},{10,11... | collective-permute-start | bytes 6152 | tf_op jit(solution)/shard_map/ppermute | solution.py:23
  21.2 3.0 %collective-permute-start.9 = (f32[2,256]{1,0:T(2,128)S(1)}, f32[2,256]{1,0:T(2,128)S(1)}, u32[]{:S(2)}, u32[]{:S(2)}) collective-permute-start(f32[2,256]{1,0:T(2,128)S(1)} %add.14), channel_id=1, source_target_pairs={{0,9},{1,8},{2,11},{3,10},{4,13},{5,12},{6,15},{7,14},{8,1},{9,0},... | collective-permute-start | bytes 6152 | tf_op jit(solution)/shard_map/ppermute | solution.py:234
  24.3 3.9 %collective-permute-start.10 = (f32[2,256]{1,0:T(2,128)S(1)}, f32[2,256]{1,0:T(2,128)S(1)}, u32[]{:S(2)}, u32[]{:S(2)}) collective-permute-start(f32[2,256]{1,0:T(2,128)S(1)} %add.15), channel_id=1, source_target_pairs={{0,17},{1,16},{2,19},{3,18},{4,21},{5,20},{6,23},{7,22},{8,25},{9,... | collective-permute-start | bytes 6152 | tf_op jit(solution)/shard_map/ppermute | solution.py:234

commit v3 on v2

--- a/solution.py
+++ b/solution.py
@@ -38,7 +38,7 @@
     for i in range(PARTS):
         part = pl.ds(i * step, step)
         copies.append(pltpu.make_async_copy(feat_ref.at[part], msg_ref.at[part], sem.at[2 + i]))
-    for copy in copies:
+    for copy in copies[2:] + copies[:2]:
         copy.start()
     copies[0].wait()
     ids = ids_buf[...]
@@ -169,8 +169,11 @@
     half_ref[states:] = precs
     mean_f = means.astype(jnp.float32)
     prec_f = precs.astype(jnp.float32)
-    product = (mean_f * prec_f).astype(jnp.bfloat16)
-    constant = jnp.sum(mean_f * product.astype(jnp.float32) - jnp.log(prec_f), axis=1, keepdims=True)
+    product = means * precs
+    half = width // 2
+    paired = mean_f * product.astype(jnp.float32)
+    logs = jnp.log(prec_f[:, :half] * prec_f[:, half:])
+    constant = jnp.sum(paired[:, :half] + paired[:, half:] - logs, axis=1, keepdims=True)
     table_ref[:, :width] = product * jnp.bfloat16(-2.0)
     table_ref[:, width:] = precs
     likely = lax.dot_general(table_ref[...], both_ref[...], (((1,), (1,)), ((), ())), preferred_element_type=jnp.float32)
@@ -249,8 +252,7 @@
     near = swap(own, "states", 1)
     back = [swap(v, "states", 1) for v in far]
     total, occ, post, both = moments([own, near], topk, states, ())
-    old = moments([far[0]], topk, states, (total, occ))
-    old = moments([back[0]], topk, states, old)
+    old = moments([far[0], back[0]], topk, states, (total, occ))
     old = moments([far[1]], topk, states, old)
     old = moments([back[1], far[2]], topk, states, old)
     half, score = final([back[2]], topk, own, near, post, both, old, width * depth)

time: 29.8 us -> 29.6 us (level)
    pallas_call x5 -> x4, Pallas kernels: 4.7 us -> 4.52 us  [moments(): pl.pallas_call(functools.partial(moments_kernel, n, topk, first), out_sha...]
  transfers between devices with their start and end apart: 11 -> 11, of which waited for: 6 -> 6; matrix products, arithmetic and copies ran while one was open for 2% -> 2% of each run, Pallas kernels for 16% -> 15%
where the time goes in v3:
time: 29.6 us; the launch traced here: 29.4 us
  waiting for transfers between devices  11.3 us (38%)
  starting transfers between devices  9.54 us (32%)
  Pallas kernels  7.38 us (25%)
  between operations  0.66 us (2%)
  other arithmetic  0.58 us (2%)
    ppermute x9, waiting for transfers between devices, swap(): return lax.ppermute(value, axis, [(i, i ^ k) for i in range(n)])  8.47 us
    ppermute x9, starting transfers between devices, swap(): return lax.ppermute(value, axis, [(i, i ^ k) for i in range(n)])  5.41 us
    pallas_call x4, Pallas kernels, moments(): pl.pallas_call(functools.partial(moments_kernel, n, topk, first), out_sha...  4.52 us
    ppermute x2, starting transfers between devices, hop(): return lax.ppermute(value, ('frames', 'states'), pairs)  4.12 us
    ppermute x2, waiting for transfers between devices, hop(): return lax.ppermute(value, ('frames', 'states'), pairs)  2.8 us
    pallas_call x1, Pallas kernels, final(): pl.pallas_call(functools.partial(final_kernel, n, topk, float(full_width)...  1.06 us
    pallas_call x1, Pallas kernels, place(): pl.pallas_call(place_kernel, out_shape=(out, out), in_specs=vmem(2), out_...  0.9 us
    pallas_call x1, Pallas kernels, prep(): pl.pallas_call(prep_kernel, out_shape=jax.ShapeDtypeStruct((rows + 2 * to...  0.9 us
  transfers between devices with their start and end apart: 11, of which 6 were waited for; matrix products, arithmetic and copies ran while one was open for 2% of the time, Pallas kernels for 15%

profile of v3, /device:TPU:0, one launch (start us, length us, event | category | flops | bytes accessed | tf_op | source)
XLA Modules:
  0.0 29.4 jit_solution(5131251702987422298)
XLA Ops:
  0.6 0.9 %prep.1.refs_0_.refs_1_ = bf16[320,256]{1,0:T(8,128)(2,1)S(1)} custom-call(bf16[256,256]{1,0:T(8,128)(2,1)} %feat_ref.1, s32[32,256]{1,0:T(8,128)} %bitcast.3, f32[32,256]{1,0:T(8,128)} %bitcast.4), custom_call_target="tpu_custom_call" | custom-call | tf_op jit(solution)/shard_map/prep/pallas_call | solution.py:56
  1.5 3.1 %collective-permute-start.5 = (bf16[320,256]{1,0:T(8,128)(2,1)S(1)}, bf16[320,256]{1,0:T(8,128)(2,1)S(1)}, u32[]{:S(2)}, u32[]{:S(2)}) collective-permute-start(bf16[320,256]{1,0:T(8,128)(2,1)S(1)} %prep.1.refs_0_.refs_1_), channel_id=1, source_target_pairs={{0,4},{1,5},{2,6},{3,7},{4,0},{5,1},{6,2},{7,3},{8,12},{9,13},{10,... | collective-permute-start | bytes 491528 | tf_op jit(solution)/shard_map/ppermute | solution.py:23
  4.6 1.5 %collective-permute-start.3 = (bf16[320,256]{1,0:T(8,128)(2,1)S(1)}, bf16[320,256]{1,0:T(8,128)(2,1)S(1)}, u32[]{:S(2)}, u32[]{:S(2)}) collective-permute-start(bf16[320,256]{1,0:T(8,128)(2,1)S(1)} %prep.1.refs_0_.refs_1_), channel_id=1, source_target_pairs={{0,2},{1,3},{2,0},{3,1},{4,6},{5,7},{6,4},{7,5},{8,10},{9,11},{10,... | collective-permute-start | bytes 491528 | tf_op jit(solution)/shard_map/ppermute | solution.py:23
  6.1 0.0 collective-permute-start
  6.1 0.2 collective-permute-start.2
  6.3 2.5 %collective-permute-done.5.refs_0_ = bf16[320,256]{1,0:T(8,128)(2,1)S(1)} collective-permute-done((bf16[320,256]{1,0:T(8,128)(2,1)S(1)}, bf16[320,256]{1,0:T(8,128)(2,1)S(1)}, u32[]{:S(2)}, u32[]{:S(2)}) %collective-permute-start.5) | collective-permute-done | bytes 163872 | tf_op jit(solution)/shard_map/ppermute | solution.py:23
  8.8 0.0 collective-permute-start.6
  8.8 2.7 %collective-permute-done.3.refs_0_ = bf16[320,256]{1,0:T(8,128)(2,1)S(1)} collective-permute-done((bf16[320,256]{1,0:T(8,128)(2,1)S(1)}, bf16[320,256]{1,0:T(8,128)(2,1)S(1)}, u32[]{:S(2)}, u32[]{:S(2)}) %collective-permute-start.3) | collective-permute-done | bytes 163872 | tf_op jit(solution)/shard_map/ppermute | solution.py:23
  11.5 0.0 collective-permute-start.4
  11.5 2.0 %collective-permute-done.refs_1_ = bf16[320,256]{1,0:T(8,128)(2,1)S(1)} collective-permute-done((bf16[320,256]{1,0:T(8,128)(2,1)S(1)}, bf16[320,256]{1,0:T(8,128)(2,1)S(1)}, u32[]{:S(2)}, u32[]{:S(2)}) %collective-permute-start) | collective-permute-done | bytes 163872 | tf_op jit(solution)/shard_map/ppermute | solution.py:23
  13.5 0.1 collective-permute-start.1
  13.6 0.0 collective-permute-done.2.refs_1_.refs_2_
  13.6 1.2 %shard_map.58 = (f32[384,512]{1,0:T(8,128)S(1)}, f32[384,128]{1,0:T(8,128)S(1)}, bf16[384,512]{1,0:T(8,128)(2,1)S(1)}, bf16[512,512]{1,0:T(8,128)(2,1)S(1)}) custom-call(bf16[320,256]{1,0:T(8,128)(2,1)S(1)} %prep.1.refs_0_.refs_1_, bf16[320,256]{1,0:T(8,128)(2,1)S(1)} %collective-permute-done.2.refs_1_.refs_2_), custom_call_target="tpu_custom_call" | custom-call | flops 786432000 | bytes 1048576 | tf_op jit(solution)/shard_map/pallas_call | solution.py:142
  14.9 0.0 collective-permute-done.6.refs_1_
  14.9 1.3 %shard_map.59 = (f32[384,512]{1,0:T(8,128)S(1)}, f32[384,128]{1,0:T(8,128)S(1)}) custom-call(bf16[320,256]{1,0:T(8,128)(2,1)S(1)} %collective-permute-done.5.refs_0_, bf16[320,256]{1,0:T(8,128)(2,1)S(1)} %collective-permute-done.6.refs_1_, f32[384,512]{1,0:T(8,128)S(1)} %get-tuple-element.19.refs_2_, f32[384,128]{1,0:T(8,128)S(1)} %get-tuple-element.20.refs_3_), custom_call_target="tpu_custom_call" | custom-call | flops 786432000 | bytes 1048576 | tf_op jit(solution)/shard_map/pallas_call | solution.py:142
  16.1 0.7 %shard_map.60 = (f32[384,512]{1,0:T(8,128)S(1)}, f32[384,128]{1,0:T(8,128)S(1)}) custom-call(bf16[320,256]{1,0:T(8,128)(2,1)S(1)} %collective-permute-done.3.refs_0_, f32[384,512]{1,0:T(8,128)S(1)} %get-tuple-element.21.refs_1_, f32[384,128]{1,0:T(8,128)S(1)} %get-tuple-element.22.refs_2_), custom_call_target="tpu_custom_call" | custom-call | flops 393216000 | bytes 1048576 | tf_op jit(solution)/shard_map/pallas_call | solution.py:142
  16.9 0.0 collective-permute-done.4.refs_0_
  16.9 1.3 %shard_map.61 = (f32[384,512]{1,0:T(8,128)S(1)}, f32[384,128]{1,0:T(8,128)S(1)}) custom-call(bf16[320,256]{1,0:T(8,128)(2,1)S(1)} %collective-permute-done.4.refs_0_, bf16[320,256]{1,0:T(8,128)(2,1)S(1)} %collective-permute-done.refs_1_, f32[384,512]{1,0:T(8,128)S(1)} %get-tuple-element.23.refs_2_, f32[384,128]{1,0:T(8,128)S(1)} %get-tuple-element.24.refs_3_), custom_call_target="tpu_custom_call" | custom-call | flops 786432000 | bytes 1048576 | tf_op jit(solution)/shard_map/pallas_call | solution.py:142
  18.1 0.0 collective-permute-done.1.refs_0_
  18.1 1.1 %final.1 = (bf16[768,256]{1,0:T(8,128)(2,1)S(1)}, f32[2,256]{1,0:T(2,128)S(1)}) custom-call(bf16[320,256]{1,0:T(8,128)(2,1)S(1)} %collective-permute-done.1.refs_0_, bf16[320,256]{1,0:T(8,128)(2,1)S(1)} %prep.1.refs_0_.refs_1_, bf16[320,256]{1,0:T(8,128)(2,1)S(1)} %collective-permute-done.2.refs_1_.refs_2_, bf16[384,512]{1,0:T(8,128)(2,1)S(1)} %get-tuple-element.17.refs_3_, ...), custom_call_target="tpu_custom_call" | custom-call | flops 805306368 | bytes 4194304 | tf_op jit(solution)/shard_map/final/pallas_call | solution.py:192
  19.2 0.5 %collective-permute-start.7 = (bf16[768,256]{1,0:T(8,128)(2,1)S(1)}, bf16[768,256]{1,0:T(8,128)(2,1)S(1)}, u32[]{:S(2)}, u32[]{:S(2)}) collective-permute-start(bf16[768,256]{1,0:T(8,128)(2,1)S(1)} %get-tuple-element.27.mine_ref), channel_id=1, source_target_pairs={{0,1},{1,0},{2,3},{3,2},{4,5},{5,4},{6,7},{7,6},{8,9},{9,8},{10,11... | collective-permute-start | bytes 1179656 | tf_op jit(solution)/shard_map/ppermute | solution.py:23
  19.7 0.1 collective-permute-start.8
  19.8 1.2 %collective-permute-done.8 = f32[2,256]{1,0:T(2,128)S(1)} collective-permute-done((f32[2,256]{1,0:T(2,128)S(1)}, f32[2,256]{1,0:T(2,128)S(1)}, u32[]{:S(2)}, u32[]{:S(2)}) %collective-permute-start.8) | collective-permute-done | bytes 2080 | tf_op jit(solution)/shard_map/ppermute | solution.py:23
  21.0 1.6 %collective-permute-start.9 = (f32[2,256]{1,0:T(2,128)S(1)}, f32[2,256]{1,0:T(2,128)S(1)}, u32[]{:S(2)}, u32[]{:S(2)}) collective-permute-start(f32[2,256]{1,0:T(2,128)S(1)} %add.14), channel_id=1, source_target_pairs={{0,9},{1,8},{2,11},{3,10},{4,13},{5,12},{6,15},{7,14},{8,1},{9,0},... | collective-permute-start | bytes 6152 | tf_op jit(solution)/shard_map/ppermute | solution.py:237
  22.6 1.5 %collective-permute-done.9 = f32[2,256]{1,0:T(2,128)S(1)} collective-permute-done((f32[2,256]{1,0:T(2,128)S(1)}, f32[2,256]{1,0:T(2,128)S(1)}, u32[]{:S(2)}, u32[]{:S(2)}) %collective-permute-start.9) | collective-permute-done | bytes 2080 | tf_op jit(solution)/shard_map/ppermute | solution.py:237
  24.0 2.6 %collective-permute-start.10 = (f32[2,256]{1,0:T(2,128)S(1)}, f32[2,256]{1,0:T(2,128)S(1)}, u32[]{:S(2)}, u32[]{:S(2)}) collective-permute-start(f32[2,256]{1,0:T(2,128)S(1)} %add.15), channel_id=1, source_target_pairs={{0,17},{1,16},{2,19},{3,18},{4,21},{5,20},{6,23},{7,22},{8,25},{9,... | collective-permute-start | bytes 6152 | tf_op jit(solution)/shard_map/ppermute | solution.py:237
  26.6 1.3 %collective-permute-done.10 = f32[2,256]{1,0:T(2,128)S(1)} collective-permute-done((f32[2,256]{1,0:T(2,128)S(1)}, f32[2,256]{1,0:T(2,128)S(1)}, u32[]{:S(2)}, u32[]{:S(2)}) %collective-permute-start.10) | collective-permute-done | bytes 2080 | tf_op jit(solution)/shard_map/ppermute | solution.py:237
  27.9 0.6 %broadcast_select_fusion = f32[1,256]{1,0:T(1,128)} fusion(pred[]{:T(512)S(6)} %eq.5, f32[2,256]{1,0:T(2,128)S(1)} %add.16), kind=kLoop, calls=%fused_computation | loop fusion | flops 256 | bytes 3073 | tf_op jit(solution)/shard_map/jit(_where)/select_n | solution.py:267
  28.5 0.0 collective-permute-done.7.other_ref
  28.5 0.9 %place.1 = (bf16[768,256]{1,0:T(8,128)(2,1)}, bf16[768,256]{1,0:T(8,128)(2,1)}) custom-call(bf16[768,256]{1,0:T(8,128)(2,1)S(1)} %get-tuple-element.27.mine_ref, bf16[768,256]{1,0:T(8,128)(2,1)S(1)} %collective-permute-done.7.other_ref), custom_call_target="tpu_custom_call" | custom-call | flops 1048576 | bytes 1048576 | tf_op jit(solution)/shard_map/place/pallas_call | solution.py:224
  (3 shorter events, 0.0 us)
Async XLA Ops:
  1.5 7.3 %collective-permute-start.5 = (bf16[320,256]{1,0:T(8,128)(2,1)S(1)}, bf16[320,256]{1,0:T(8,128)(2,1)S(1)}, u32[]{:S(2)}, u32[]{:S(2)}) collective-permute-start(bf16[320,256]{1,0:T(8,128)(2,1)S(1)} %prep.1.refs_0_.refs_1_), channel_id=1, source_target_pairs={{0,4},{1,5},{2,6},{3,7},{4,0},{5,1},{6,2},{7,3},{8,12},{9,13},{10,... | collective-permute-start | bytes 491528 | tf_op jit(solution)/shard_map/ppermute | solution.py:23
  4.6 6.9 %collective-permute-start.3 = (bf16[320,256]{1,0:T(8,128)(2,1)S(1)}, bf16[320,256]{1,0:T(8,128)(2,1)S(1)}, u32[]{:S(2)}, u32[]{:S(2)}) collective-permute-start(bf16[320,256]{1,0:T(8,128)(2,1)S(1)} %prep.1.refs_0_.refs_1_), channel_id=1, source_target_pairs={{0,2},{1,3},{2,0},{3,1},{4,6},{5,7},{6,4},{7,5},{8,10},{9,11},{10,... | collective-permute-start | bytes 491528 | tf_op jit(solution)/shard_map/ppermute | solution.py:23
  6.1 7.4 %collective-permute-start = (bf16[320,256]{1,0:T(8,128)(2,1)S(1)}, bf16[320,256]{1,0:T(8,128)(2,1)S(1)}, u32[]{:S(2)}, u32[]{:S(2)}) collective-permute-start(bf16[320,256]{1,0:T(8,128)(2,1)S(1)} %prep.1.refs_0_.refs_1_), channel_id=1, source_target_pairs={{0,7},{1,6},{2,5},{3,4},{4,3},{5,2},{6,1},{7,0},{8,15},{9,14},{10,... | collective-permute-start | bytes 491528 | tf_op jit(solution)/shard_map/ppermute | solution.py:23
  6.1 7.5 %collective-permute-start.2 = (bf16[320,256]{1,0:T(8,128)(2,1)S(1)}, bf16[320,256]{1,0:T(8,128)(2,1)S(1)}, u32[]{:S(2)}, u32[]{:S(2)}) collective-permute-start(bf16[320,256]{1,0:T(8,128)(2,1)S(1)} %prep.1.refs_0_.refs_1_), channel_id=1, source_target_pairs={{0,1},{1,0},{2,3},{3,2},{4,5},{5,4},{6,7},{7,6},{8,9},{9,8},{10,11... | collective-permute-start | bytes 491528 | tf_op jit(solution)/shard_map/ppermute | solution.py:23
  8.8 6.1 %collective-permute-start.6 = (bf16[320,256]{1,0:T(8,128)(2,1)S(1)}, bf16[320,256]{1,0:T(8,128)(2,1)S(1)}, u32[]{:S(2)}, u32[]{:S(2)}) collective-permute-start(bf16[320,256]{1,0:T(8,128)(2,1)S(1)} %collective-permute-done.5.refs_0_), channel_id=1, source_target_pairs={{0,1},{1,0},{2,3},{3,2},{4,5},{5,4},{6,7},{7,6},{8,9},{9,8},{10,11... | collective-permute-start | bytes 491528 | tf_op jit(solution)/shard_map/ppermute | solution.py:23
  11.5 5.4 %collective-permute-start.4 = (bf16[320,256]{1,0:T(8,128)(2,1)S(1)}, bf16[320,256]{1,0:T(8,128)(2,1)S(1)}, u32[]{:S(2)}, u32[]{:S(2)}) collective-permute-start(bf16[320,256]{1,0:T(8,128)(2,1)S(1)} %collective-permute-done.3.refs_0_), channel_id=1, source_target_pairs={{0,1},{1,0},{2,3},{3,2},{4,5},{5,4},{6,7},{7,6},{8,9},{9,8},{10,11... | collective-permute-start | bytes 491528 | tf_op jit(solution)/shard_map/ppermute | solution.py:23
  13.5 4.6 %collective-permute-start.1 = (bf16[320,256]{1,0:T(8,128)(2,1)S(1)}, bf16[320,256]{1,0:T(8,128)(2,1)S(1)}, u32[]{:S(2)}, u32[]{:S(2)}) collective-permute-start(bf16[320,256]{1,0:T(8,128)(2,1)S(1)} %collective-permute-done.refs_1_), channel_id=1, source_target_pairs={{0,1},{1,0},{2,3},{3,2},{4,5},{5,4},{6,7},{7,6},{8,9},{9,8},{10,11... | collective-permute-start | bytes 491528 | tf_op jit(solution)/shard_map/ppermute | solution.py:23
  19.2 9.3 %collective-permute-start.7 = (bf16[768,256]{1,0:T(8,128)(2,1)S(1)}, bf16[768,256]{1,0:T(8,128)(2,1)S(1)}, u32[]{:S(2)}, u32[]{:S(2)}) collective-permute-start(bf16[768,256]{1,0:T(8,128)(2,1)S(1)} %get-tuple-element.27.mine_ref), channel_id=1, source_target_pairs={{0,1},{1,0},{2,3},{3,2},{4,5},{5,4},{6,7},{7,6},{8,9},{9,8},{10,11... | collective-permute-start | bytes 1179656 | tf_op jit(solution)/shard_map/ppermute | solution.py:23
  19.7 1.4 %collective-permute-start.8 = (f32[2,256]{1,0:T(2,128)S(1)}, f32[2,256]{1,0:T(2,128)S(1)}, u32[]{:S(2)}, u32[]{:S(2)}) collective-permute-start(f32[2,256]{1,0:T(2,128)S(1)} %get-tuple-element.30), channel_id=1, source_target_pairs={{0,1},{1,0},{2,3},{3,2},{4,5},{5,4},{6,7},{7,6},{8,9},{9,8},{10,11... | collective-permute-start | bytes 6152 | tf_op jit(solution)/shard_map/ppermute | solution.py:23
  21.0 3.0 %collective-permute-start.9 = (f32[2,256]{1,0:T(2,128)S(1)}, f32[2,256]{1,0:T(2,128)S(1)}, u32[]{:S(2)}, u32[]{:S(2)}) collective-permute-start(f32[2,256]{1,0:T(2,128)S(1)} %add.14), channel_id=1, source_target_pairs={{0,9},{1,8},{2,11},{3,10},{4,13},{5,12},{6,15},{7,14},{8,1},{9,0},... | collective-permute-start | bytes 6152 | tf_op jit(solution)/shard_map/ppermute | solution.py:237
  24.0 3.9 %collective-permute-start.10 = (f32[2,256]{1,0:T(2,128)S(1)}, f32[2,256]{1,0:T(2,128)S(1)}, u32[]{:S(2)}, u32[]{:S(2)}) collective-permute-start(f32[2,256]{1,0:T(2,128)S(1)} %add.15), channel_id=1, source_target_pairs={{0,17},{1,16},{2,19},{3,18},{4,21},{5,20},{6,23},{7,22},{8,25},{9,... | collective-permute-start | bytes 6152 | tf_op jit(solution)/shard_map/ppermute | solution.py:237
